TPU v7x, 128 devices: a whole 4x4x4 slice. The times are simulated.
128 devices in a mesh: frame: 32 (over x, y, z_lo), row: 4 (over z_hi, core).
Axes of the slice: x: 4, y: 4, z: 4 (z_hi: 2, z_lo: 2; z = z_hi * 2 + z_lo), core: 2. Of those that a mesh axis runs over, the one named last changes fastest.
Arguments:
- tokens: bfloat16 [32, 512, 2048], P('frame', 'row'), may hold values from -6 to 6
- w_gate: bfloat16 [2048, 4096], P(None, 'row'), may hold values from -0.125 to 0.125
- w_value: bfloat16 [2048, 4096], P(None, 'row'), may hold values from -0.125 to 0.125
- w_state_proj: bfloat16 [2048, 512], replicated, may hold values from -0.03125 to 0.03125
- w_step: bfloat16 [2, 2048, 64], P(None, None, 'row'), may hold values from -0.125 to 0.125
- step_bias: float32 [2, 64], P(None, 'row'), may hold values from -3 to 0
- decay_rate: float32 [2, 64], P(None, 'row'), may hold values from 0 to 0.3, as said below
- conv_taps: float32 [2, 4, 4096], P(None, None, 'row'), may hold values from -3 to 3
- skip_gain: float32 [2, 64], P(None, 'row'), may hold values from 0.1 to 16, as said below
- norm_gain: float32 [4096], P('row'), may hold values from 0.1 to 1.9
- w_out: bfloat16 [4096, 2048], P('row'), may hold values from -0.09375 to 0.09375
Outputs:
- mixed: bfloat16 [32, 512, 2048], P('frame', 'row')
Inputs may be any that keep to these rules, and one draw needn't show every extreme that they name: `decay_rate`: positive decay rates. `skip_gain`: positive skip weights.
All inputs are finite; a program needn't handle non-finite values.
Results may differ from a plain program's by a relative error of at most 0.015.
Values may be sent and summed in bfloat16 or wider, within the bound.
A program may use at most 128 MiB of HBM per device.

v0:
```python
import jax
import jax.numpy as jnp
from jax import lax
from jax.sharding import Mesh
from jax.sharding import PartitionSpec as P

D_INNER = 4096
HEAD_DIM = 64
CONV = 4
BLK = 128
FRAME = ("frame_0", "frame_1", "frame_2")


def in_order(pieces, dim):
    pieces = jnp.moveaxis(pieces, 0, dim)
    shape = pieces.shape
    return pieces.reshape(*shape[:dim], shape[dim] * shape[dim + 1], *shape[dim + 2 :])


def sent_to_all(shard, axis):
    devices = lax.axis_size(axis)
    return lax.all_to_all(
        jnp.broadcast_to(shard[None], (devices, *shard.shape)), axis, 0, 0, tiled=True
    )


def gather_directly(shard, axis, dim):
    return in_order(sent_to_all(shard, axis), dim)


def with_halo(shard, sides, width):
    for axis, dim in sides:
        devices, length = (lax.axis_size(axis), shard.shape[dim])
        up = [(i, (i + 1) % devices) for i in range(devices - 1)]
        down = [(j, i) for i, j in up]
        last = lax.slice_in_dim(shard, length - width, length, axis=dim)
        initial = lax.slice_in_dim(shard, 0, width, axis=dim)
        before = lax.ppermute(last, axis, up)
        after = lax.ppermute(initial, axis, down)
        shard = jnp.concatenate([before, shard, after], axis=dim)
    return shard


def nothing_yet(shard, identity):
    return jax.tree.map(
        lambda part, zero: jnp.zeros_like(part) + jnp.asarray(zero, part.dtype), shard, identity
    )


def entering_2(shard, axes, combine, identity, reverse):
    before = start = nothing_yet(shard, identity)
    running = shard
    for axis in reversed(axes):
        devices, mine = (lax.axis_size(axis), lax.axis_index(axis))
        pieces = jax.tree.map(
            lambda part, kind: lax.all_gather(part.astype(kind), axis),
            running,
            (jnp.bfloat16, jnp.bfloat16),
        )
        inside, running = (start, start)
        for k in reversed(range(devices)) if reverse else range(devices):
            passed = k > mine if reverse else k < mine
            running = combine(
                running, jax.tree.map(lambda part, own: part[k].astype(own.dtype), pieces, shard)
            )
            inside = jax.tree.map(lambda new, old: jnp.where(passed, new, old), running, inside)
        before = combine(inside, before)
    return before


def taken_together(shard, axis):
    return sent_to_all(shard, axis).sum(axis=0)


def split_up(shard, dim, devices):
    shape = shard.shape
    pieces = shard.reshape(*shape[:dim], devices, shape[dim] // devices, *shape[dim + 1 :])
    return jnp.moveaxis(pieces, dim, 0)


def summed_on_arrival(shard, axis, dim):
    devices = lax.axis_size(axis)
    pieces = lax.all_to_all(split_up(shard, dim, devices), axis, 0, 0, tiled=True)
    return jnp.sum(pieces.astype(jnp.float32), axis=0)


def block_weights(scores, log_cum, dt_block):
    size = scores.shape[0]
    row_index = lax.broadcasted_iota(jnp.int32, (size, size), 0)
    col_index = lax.broadcasted_iota(jnp.int32, (size, size), 1)
    causal = row_index >= col_index
    log_gap = log_cum.T[:, :, None] - log_cum.T[:, None, :]
    fading = jnp.exp(jnp.where(causal[None], log_gap, -jnp.inf))
    return (scores[None] * fading * dt_block.T[:, None, :]).astype(jnp.bfloat16)


def local_pass(values, b_rows, c_rows, dt_rows, rate_row):
    tok_count, heads_here, head_width = values.shape
    block_count = tok_count // BLK
    blocks = (
        values.reshape(block_count, BLK, heads_here, head_width),
        b_rows.reshape(block_count, BLK, -1),
        c_rows.reshape(block_count, BLK, -1),
        dt_rows.reshape(block_count, BLK, heads_here),
    )
    state_zero = jnp.zeros((heads_here, head_width, b_rows.shape[1]), jnp.float32)

    def advance(carry, block):
        carry_state, offset = carry
        x_block, b_block, c_block, dt_block = block
        log_cum = jnp.cumsum(-dt_block * rate_row[None, :], axis=0)
        scores = jnp.einsum("tn,sn->ts", c_block, b_block, preferred_element_type=jnp.float32)
        weights = block_weights(scores, log_cum, dt_block)
        inner_out = jnp.einsum("hts,shp->thp", weights, x_block, preferred_element_type=jnp.float32)
        log_last = log_cum[-1]
        carried = (
            (jnp.exp(log_last[None, :] - log_cum) * dt_block)[:, :, None]
            * x_block.astype(jnp.float32)
        ).astype(jnp.bfloat16)
        update = jnp.einsum("sn,shp->hpn", b_block, carried, preferred_element_type=jnp.float32)
        new_state = jnp.exp(log_last)[:, None, None] * carry_state + update
        return ((new_state, offset + log_last), (inner_out, log_cum, carry_state, offset))

    finals, saved = lax.scan(advance, (state_zero, jnp.zeros((heads_here,), jnp.float32)), blocks)
    return (finals, saved, blocks)


def finish(saved, blocks, incoming, skip_row):
    inner_out, log_cum, starts, offsets = saved
    x_blocks, unused_b, c_blocks, unused_dt = blocks
    entering = (starts + jnp.exp(offsets)[:, :, None, None] * incoming[None]).astype(jnp.bfloat16)
    carried_out = jnp.einsum(
        "btn,bhpn->bthp", c_blocks, entering, preferred_element_type=jnp.float32
    )
    result = (
        inner_out
        + carried_out * jnp.exp(log_cum)[..., None]
        + skip_row[None, None, :, None] * x_blocks.astype(jnp.float32)
    )
    return result.reshape(-1, result.shape[2], result.shape[3])


def chain_link(earlier, later):
    return (earlier[0] + later[0], jnp.exp(later[0])[:, None, None] * earlier[1] + later[1])


def conv_pass(padded, taps, tok_count, backward):
    reach = taps.shape[0] - 1
    running = jnp.zeros((tok_count, padded.shape[1]), jnp.float32)
    for tap_index in range(taps.shape[0]):
        first_row = 2 * reach - tap_index if backward else tap_index
        running = running + taps[tap_index][None, :] * padded[first_row : first_row + tok_count]
    return jax.nn.silu(running).astype(jnp.bfloat16)


def per_device(
    tokens,
    w_gate,
    w_value,
    w_state_proj,
    w_step,
    step_bias,
    decay_rate,
    conv_taps,
    skip_gain,
    norm_gain,
    w_out,
):
    channels = w_gate.shape[1]
    heads_here = step_bias.shape[1]
    state_size = w_state_proj.shape[1] // 4
    shard_piece = gather_directly(tokens, "row", 1)
    matrices = (w_gate, w_value, w_state_proj, w_step[0], w_step[1])
    outputs = [
        jnp.einsum("frd,dk->frk", shard_piece, matrix, preferred_element_type=jnp.float32).astype(
            jnp.bfloat16
        )
        for matrix in matrices
    ]
    projected = jnp.concatenate(outputs, axis=2)
    frame_count, patch_count = (projected.shape[0], projected.shape[1])
    tok_count = frame_count * patch_count
    projected = projected.reshape(tok_count, -1)
    gate_in = projected[:, :channels]
    x_raw = projected[:, channels : 2 * channels]
    edge = 2 * channels + 4 * state_size
    bc_cols = projected[:, 2 * channels : edge]
    dt_forward = jax.nn.softplus(
        projected[:, edge : edge + heads_here].astype(jnp.float32) + step_bias[0][None, :]
    )
    dt_backward = jax.nn.softplus(
        projected[:, edge + heads_here : edge + 2 * heads_here].astype(jnp.float32)
        + step_bias[1][None, :]
    )
    padded = with_halo(x_raw, ((FRAME, 0),), CONV - 1).astype(jnp.float32)
    shape_heads = (tok_count, heads_here, HEAD_DIM)
    x_forward = conv_pass(padded, conv_taps[0], tok_count, False).reshape(shape_heads)
    x_backward = conv_pass(padded, conv_taps[1], tok_count, True).reshape(shape_heads)
    finals_fwd, saved_fwd, blocks_fwd = local_pass(
        x_forward,
        bc_cols[:, :state_size],
        bc_cols[:, state_size : 2 * state_size],
        dt_forward,
        decay_rate[0],
    )
    finals_bwd, saved_bwd, blocks_bwd = local_pass(
        jnp.flip(x_backward, 0),
        jnp.flip(bc_cols[:, 2 * state_size : 3 * state_size], 0),
        jnp.flip(bc_cols[:, 3 * state_size :], 0),
        jnp.flip(dt_backward, 0),
        decay_rate[1],
    )
    empty_pair = (
        jnp.zeros((heads_here,), jnp.float32),
        jnp.zeros((heads_here, HEAD_DIM, state_size), jnp.float32),
    )
    entry_fwd = entering_2((finals_fwd[1], finals_fwd[0]), FRAME, chain_link, empty_pair, False)[1]
    entry_bwd = entering_2((finals_bwd[1], finals_bwd[0]), FRAME, chain_link, empty_pair, True)[1]
    y_forward = finish(saved_fwd, blocks_fwd, entry_fwd, skip_gain[0])
    y_backward = jnp.flip(finish(saved_bwd, blocks_bwd, entry_bwd, skip_gain[1]), 0)
    summed = (y_forward + y_backward).reshape(tok_count, channels)
    gated = summed * jax.nn.silu(gate_in.astype(jnp.float32))
    local_squares = jnp.sum(gated * gated, axis=-1)
    total_squares = taken_together(local_squares, "row")
    scale = lax.rsqrt(total_squares / D_INNER + 1e-05)
    normed = (gated * scale[:, None] * norm_gain[None, :]).astype(jnp.bfloat16)
    normed = normed.reshape(frame_count, patch_count, channels)
    partial_value = jnp.einsum("fpc,cd->fpd", normed, w_out, preferred_element_type=jnp.float32)
    reduced = summed_on_arrival(
        jnp.transpose(partial_value, (1, 0, 2)).astype(jnp.bfloat16), "row", 0
    )
    mixed = jnp.transpose(reduced, (1, 0, 2)).astype(jnp.bfloat16)
    return mixed


def solution(mesh):
    finer = Mesh(
        mesh.devices.reshape(4, 4, 2, mesh.shape["row"]), ("frame_0", "frame_1", "frame_2", "row")
    )
    in_specs = (
        P(FRAME, "row", None),
        P(None, "row"),
        P(None, "row"),
        P(),
        P(None, None, "row"),
        P(None, "row"),
        P(None, "row"),
        P(None, None, "row"),
        P(None, "row"),
        P("row"),
        P("row", None),
    )
    out_specs = P(FRAME, "row", None)
    return jax.shard_map(
        per_device, mesh=finer, in_specs=in_specs, out_specs=out_specs, check_vma=False
    )
```

profile of v0, /device:TPU:1, one launch (start us, length us, event | category | flops | bytes accessed | tf_op | source)
XLA Modules:
  0.0 324.9 jit_solution(4357447601501778239)
XLA Ops:
  6.5 2.8 broadcast_in_dim.69
  9.4 6.8 %all-to-all-start = ((bf16[4,1,128,2048]{3,2,1,0:T(8,128)(2,1)}), bf16[4,1,128,2048]{3,2,1,0:T(8,128)(2,1)}, u32[]{:S(2)}, u32[]{:S(2)}) async-start(bf16[4,1,128,2048]{3,2,1,0:T(8,128)(2,1)} %broadcast_in_dim.69), calls=%async_computation | async-start | bytes 4194304 | tf_op jit(solution)/shard_map/all_to_all | solution.py:22
  18.1 24.4 %all-to-all-done = bf16[4,1,128,2048]{3,2,1,0:T(8,128)(2,1)} async-done(((bf16[4,1,128,2048]{3,2,1,0:T(8,128)(2,1)}), bf16[4,1,128,2048]{3,2,1,0:T(8,128)(2,1)}, u32[]{:S(2)}, u32[]{:S(2)}) %all-to-all-start) | async-done | bytes 2097184 | tf_op jit(solution)/shard_map/all_to_all | solution.py:22
  42.5 5.3 %fusion.67 = bf16[1,512,2592]{1,2,0:T(8,128)(2,1)S(1)} fusion(bf16[512,2048]{1,0:T(8,128)(2,1)} %bitcast.1, bf16[2048,1024]{1,0:T(8,128)(2,1)} %param.16), kind=kOutput, calls=%fused_computation.110 | convolution fusion | flops 2148007936 | bytes 7340032 | tf_op jit(solution)/shard_map/frd,dk->frk/dot_general | solution.py:175
  47.8 4.0 %fusion.69 = bf16[1,512,2592]{1,2,0:T(8,128)(2,1)S(1)} fusion(bf16[1,512,2592]{1,2,0:T(8,128)(2,1)S(1)} %fusion.67, bf16[512,2048]{1,0:T(8,128)(2,1)} %bitcast.1, bf16[2048,1024]{1,0:T(8,128)(2,1)S(1)} %copy-done.54), kind=kOutput, calls=%fused_computation.112 | convolution fusion | flops 2148007936 | bytes 7340032 | tf_op jit(solution)/shard_map/frd,dk->frk/dot_general | solution.py:175
  51.8 2.9 fusion.71
  62.3 4.7 %collective-permute-start = (bf16[3,1024]{0,1:T(8,128)(2,1)}, bf16[3,1024]{0,1:T(8,128)(2,1)}, u32[]{:S(2)}, u32[]{:S(2)}) collective-permute-start(bf16[3,1024]{0,1:T(8,128)(2,1)} %get-tuple-element.429), channel_id=1, source_target_pairs={{0,4},{4,8},{8,12},{12,16},{16,20},{20,24},{24,28},{28,32},{32,36}... | collective-permute-start | bytes 18440 | tf_op jit(solution)/shard_map/ppermute | solution.py:38
  70.9 5.8 %collective-permute-done = bf16[3,1024]{0,1:T(8,128)(2,1)} collective-permute-done((bf16[3,1024]{0,1:T(8,128)(2,1)}, bf16[3,1024]{0,1:T(8,128)(2,1)}, u32[]{:S(2)}, u32[]{:S(2)}) %collective-permute-start) | collective-permute-done | bytes 6176 | tf_op jit(solution)/shard_map/ppermute | solution.py:38
  78.4 5.8 %multiply_convert_fusion.8 = (bf16[512,1024]{0,1:T(8,128)(2,1)}, bf16[512,1024]{0,1:T(8,128)(2,1)}) fusion(f32[518,1024]{0,1:T(8,128)S(1)} %maximum_convert_fusion, f32[1024]{0:T(1024)S(1)} %bitcast.399, f32[1024]{0:T(1024)S(1)} %bitcast.400, f32[1024]{0:T(1024)S(1)} %bitcast.401, f32[1024]{0:T(1024)S(1)} %bitcast.396, f32[1024]{0:T(1024)S(1)} %bitcast.402, ...), kind=kLoop, calls=%fused_computation.106 | loop fusion | flops 12582912 | bytes 16809984 | tf_op jit(solution)/shard_map/convert_element_type | solution.py:153
  84.1 2.5 rev.20
  91.1 20.3 %while.43 = (s32[]{:T(128)}, f32[16,64,128]{2,1,0:T(8,128)S(1)}, f32[16]{0:T(128)S(1)}, f32[4,128,16,64]{1,3,2,0:T(8,128)}, f32[4,128,16]{2,1,0:T(8,128)S(1)}, /...) while((s32[]{:T(128)}, f32[16,64,128]{2,1,0:T(8,128)S(1)}, ...), condition=%wide.region_5.6_spmd.clone, body=%wide.region_3.5_spmd.clone.sunk | while | flops 73816096 | bytes 3699580 | solution.py:124
  109.0 2.3 fusion.187
  118.8 25.8 %while.42 = (s32[]{:T(128)}, f32[16,64,128]{2,1,0:T(8,128)S(1)}, f32[16]{0:T(128)S(1)}, f32[4,128,16,64]{1,3,2,0:T(8,128)}, f32[4,128,16]{2,1,0:T(8,128)}, /*ind...) while((s32[]{:T(128)}, f32[16,64,128]{2,1,0:T(8,128)S(1)}, ...), condition=%wide.region_2.3_spmd.clone, body=%wide.region_0.2_spmd.clone.sunk | while | flops 73816096 | bytes 3642236 | solution.py:124
  145.1 4.5 %all-reduce.2 = (bf16[32]{0:T(256)(128)(2,1)S(1)}, bf16[32]{0:T(256)(128)(2,1)S(1)}) all-reduce(bf16[32]{0:T(256)(128)(2,1)S(1)} %dynamic-update-slice.1, bf16[32]{0:T(256)(128)(2,1)S(1)} %dynamic-update-slice), channel_id=4, replica_groups=mesh['frame_0'=4,'frame_1'=4,'frame_2'=2,'row'=4] {'frame_2'}, use_global_device_ids=true, to_apply=%add.1 | all-reduce | flops 64 | bytes 256
  149.7 7.2 %all-gather.3 = bf16[32,64,128]{2,1,0:T(8,128)(2,1)S(1)} all-gather(bf16[16,64,128]{2,1,0:T(8,128)(2,1)S(1)} %convert_element_type.518), channel_id=5, replica_groups=mesh['frame_0'=4,'frame_1'=4,'frame_2'=2,'row'=4] {'frame_2'}, dimensions={0}, use_global_device_ids=true | all-gather | bytes 786432 | tf_op jit(solution)/shard_map/all_gather | solution.py:56
  158.0 6.3 %all-gather.1 = bf16[32,64,128]{2,1,0:T(8,128)(2,1)S(1)} all-gather(bf16[16,64,128]{2,1,0:T(8,128)(2,1)S(1)} %convert_element_type.488), channel_id=3, replica_groups=mesh['frame_0'=4,'frame_1'=4,'frame_2'=2,'row'=4] {'frame_2'}, dimensions={0}, use_global_device_ids=true | all-gather | bytes 786432 | tf_op jit(solution)/shard_map/all_gather | solution.py:56
  165.5 8.0 %all-gather.6 = bf16[4,1,16]{2,1,0:T(2,128)(2,1)S(1)} all-gather(bf16[1,1,16]{2,1,0:T(2,128)(2,1)S(1)} %get-tuple-element.469), channel_id=1, replica_groups=mesh['frame_0'=4,'frame_1'=4,'frame_2'=2,'row'=4] {'frame_1'}, dimensions={0}, use_global_device_ids=true | all-gather | bytes 160 | tf_op jit(solution)/shard_map/all_gather | solution.py:56
  174.1 8.4 %all-gather.17.cloned.1.call-done = bf16[4,16,64,128]{3,2,1,0:T(8,128)(2,1)} async-done(((bf16[1,16,64,128]{3,2,1,0:T(8,128)(2,1)}), bf16[4,16,64,128]{3,2,1,0:T(8,128)(2,1)}) %all-gather.17.cloned.1.call-update) | async-done | bytes 1048592 | tf_op jit(solution)/shard_map/all_gather | solution.py:56
  184.9 6.9 %all-gather.4 = bf16[4,1,16]{2,1,0:T(2,128)(2,1)S(1)} all-gather(bf16[1,1,16]{2,1,0:T(2,128)(2,1)S(1)} %get-tuple-element.466), channel_id=1, replica_groups=mesh['frame_0'=4,'frame_1'=4,'frame_2'=2,'row'=4] {'frame_1'}, dimensions={0}, use_global_device_ids=true | all-gather | bytes 160 | tf_op jit(solution)/shard_map/all_gather | solution.py:56
  192.5 16.2 %all-gather.13.cloned.1.call-done = bf16[4,16,64,128]{3,2,1,0:T(8,128)(2,1)} async-done(((bf16[1,16,64,128]{3,2,1,0:T(8,128)(2,1)}), bf16[4,16,64,128]{3,2,1,0:T(8,128)(2,1)}) %all-gather.13.cloned.1.call-update) | async-done | bytes 1048592 | tf_op jit(solution)/shard_map/all_gather | solution.py:56
  211.5 7.6 %all-gather.7 = bf16[4,1,16]{2,1,0:T(2,128)(2,1)S(1)} all-gather(bf16[1,1,16]{2,1,0:T(2,128)(2,1)S(1)} %get-tuple-element.454), channel_id=1, replica_groups=mesh['frame_0'=4,'frame_1'=4,'frame_2'=2,'row'=4] {'frame_0'}, dimensions={0}, use_global_device_ids=true | all-gather | bytes 160 | tf_op jit(solution)/shard_map/all_gather | solution.py:56
  219.2 5.4 %all-gather.5 = bf16[4,1,16]{2,1,0:T(2,128)(2,1)S(1)} all-gather(bf16[1,1,16]{2,1,0:T(2,128)(2,1)S(1)} %get-tuple-element.445), channel_id=1, replica_groups=mesh['frame_0'=4,'frame_1'=4,'frame_2'=2,'row'=4] {'frame_0'}, dimensions={0}, use_global_device_ids=true | all-gather | bytes 160 | tf_op jit(solution)/shard_map/all_gather | solution.py:56
  231.0 3.8 %all-gather.19.cloned.1.call-done = bf16[4,16,64,128]{3,2,1,0:T(8,128)(2,1)} async-done(((bf16[1,16,64,128]{3,2,1,0:T(8,128)(2,1)}), bf16[4,16,64,128]{3,2,1,0:T(8,128)(2,1)}) %all-gather.19.cloned.1.call-update) | async-done | bytes 1048592 | tf_op jit(solution)/shard_map/all_gather | solution.py:56
  234.8 3.4 %fusion.87 = f32[16,64,128]{2,1,0:T(8,128)S(1)} fusion(bf16[4,16,64,128]{3,2,1,0:T(8,128)(2,1)} %all-gather.19.cloned.1.call-done, f32[16]{0:T(128)} %copy-done.48, f32[16]{0:T(128)} %copy-done.47, f32[16]{0:T(128)S(1)} %exponential_bitcast_fusion.6, f32[16]{0:T(128)} %copy-done.42, f32[16]{0:T(128)} %copy-done.41, f32[16]{0:T(128)} %copy-done.40, ...), kind=kLoop, calls=%fused_computation.137 | loop fusion | flops 5373952 | bytes 3146506 | tf_op jit(solution)/shard_map/mul | solution.py:131
  239.9 2.5 rev.23
  242.5 18.3 %all-gather.15.cloned.1.call-done = bf16[4,16,64,128]{3,2,1,0:T(8,128)(2,1)} async-done(((bf16[1,16,64,128]{3,2,1,0:T(8,128)(2,1)}), bf16[4,16,64,128]{3,2,1,0:T(8,128)(2,1)}) %all-gather.15.cloned.1.call-update) | async-done | bytes 1048592 | tf_op jit(solution)/shard_map/all_gather | solution.py:56
  260.8 3.2 fusion.93
  264.1 2.5 add_bitcast_fusion.1
  268.9 11.6 %all_to_all.16 = f32[4,1,512]{2,1,0:T(1,128)S(1)} all-to-all(f32[4,1,512]{2,1,0:T(1,128)S(1)} %broadcast_in_dim.70), channel_id=1, replica_groups=mesh['frame_0'=4,'frame_1'=4,'frame_2'=2,'row'=4] {'row'}, dimensions={0} | all-to-all | bytes 16384 | tf_op jit(solution)/shard_map/all_to_all | solution.py:22
  280.5 4.7 %convolution_convert_fusion = bf16[512,2048]{1,0:T(8,128)(2,1)S(1)} fusion(bf16[1024,2048]{1,0:T(8,128)(2,1)} %param.25, f32[512,1024]{0,1:T(8,128)S(1)} %get-tuple-element.412, f32[1024]{0:T(1024)S(1)} %copy-done.55, f32[512]{0:T(512)S(1)} %add_rsqrt_fusion), kind=kOutput, calls=%fused_computation.78 | convolution fusion | flops 2150105088 | bytes 8394752 | tf_op jit(solution)/shard_map/fpc,cd->fpd/dot_general | solution.py:228
  285.2 30.2 %all_to_all.17 = bf16[4,128,1,2048]{3,1,2,0:T(8,128)(2,1)} all-to-all(bf16[4,128,1,2048]{3,1,2,0:T(8,128)(2,1)S(1)} %bitcast.388), channel_id=1, replica_groups=mesh['frame_0'=4,'frame_1'=4,'frame_2'=2,'row'=4] {'row'}, dimensions={0} | all-to-all | bytes 4194304 | tf_op jit(solution)/shard_map/all_to_all | solution.py:83
  315.5 2.9 reduce_sum.32
  (326 shorter events, 89.0 us)
Async XLA Ops:
  6.5 45.3 %copy-start = (bf16[2048,512]{1,0:T(8,128)(2,1)S(1)}, bf16[2048,512]{1,0:T(8,128)(2,1)}, u32[]{:S(2)}) copy-start(bf16[2048,512]{1,0:T(8,128)(2,1)} %param.18) | copy-start | bytes 6291460
  9.4 33.1 %all-to-all-start = ((bf16[4,1,128,2048]{3,2,1,0:T(8,128)(2,1)}), bf16[4,1,128,2048]{3,2,1,0:T(8,128)(2,1)}, u32[]{:S(2)}, u32[]{:S(2)}) async-start(bf16[4,1,128,2048]{3,2,1,0:T(8,128)(2,1)} %broadcast_in_dim.69), calls=%async_computation | async-start | bytes 4194304 | tf_op jit(solution)/shard_map/all_to_all | solution.py:22
  16.1 166.4 %all-gather.17.cloned.1.call-start = ((), (), s32[]{:S(2)}) async-start(), calls=%async_computation.5 | async-start | bytes 1310720 | tf_op jit(solution)/shard_map/all_gather | solution.py:56
  61.0 9.9 %collective-permute-start.1 = (bf16[3,1024]{0,1:T(8,128)(2,1)}, bf16[3,1024]{0,1:T(8,128)(2,1)}, u32[]{:S(2)}, u32[]{:S(2)}) collective-permute-start(bf16[3,1024]{0,1:T(8,128)(2,1)} %get-tuple-element.430), channel_id=1, source_target_pairs={{4,0},{8,4},{12,8},{16,12},{20,16},{24,20},{28,24},{32,28},{36,32}... | collective-permute-start | bytes 18440 | tf_op jit(solution)/shard_map/ppermute | solution.py:39
  62.3 14.4 %collective-permute-start = (bf16[3,1024]{0,1:T(8,128)(2,1)}, bf16[3,1024]{0,1:T(8,128)(2,1)}, u32[]{:S(2)}, u32[]{:S(2)}) collective-permute-start(bf16[3,1024]{0,1:T(8,128)(2,1)} %get-tuple-element.429), channel_id=1, source_target_pairs={{0,4},{4,8},{8,12},{12,16},{16,20},{20,24},{24,28},{28,32},{32,36}... | collective-permute-start | bytes 18440 | tf_op jit(solution)/shard_map/ppermute | solution.py:38
  118.8 25.8 %copy-start.56 = (bf16[16]{0:T(256)(128)(2,1)S(1)}, bf16[16]{0:T(256)(128)(2,1)}, u32[]{:S(2)}) copy-start(bf16[16]{0:T(256)(128)(2,1)} %convert_element_type.505) | copy-start | bytes 100
  144.6 19.7 %copy-start.30 = (f32[4,16]{1,0:T(4,128)}, f32[4,16]{1,0:T(4,128)S(1)}, u32[]{:S(2)}) copy-start(f32[4,16]{1,0:T(4,128)S(1)} %get-tuple-element.141) | copy-start | bytes 772
  156.9 27.9 %copy-start.10 = (bf16[32,64,128]{2,1,0:T(8,128)(2,1)}, bf16[32,64,128]{2,1,0:T(8,128)(2,1)S(1)}, u32[]{:S(2)}) copy-start(bf16[32,64,128]{2,1,0:T(8,128)(2,1)S(1)} %all-gather.3) | copy-start | bytes 1572868
  157.9 50.8 %all-gather.13.cloned.1.call-start = ((), (), s32[]{:S(2)}) async-start(), calls=%async_computation.3 | async-start | bytes 1310720 | tf_op jit(solution)/shard_map/all_gather | solution.py:56
  164.3 46.6 %copy-start.8 = (bf16[32,64,128]{2,1,0:T(8,128)(2,1)}, bf16[32,64,128]{2,1,0:T(8,128)(2,1)S(1)}, u32[]{:S(2)}) copy-start(bf16[32,64,128]{2,1,0:T(8,128)(2,1)S(1)} %all-gather.1) | copy-start | bytes 1572868
  164.4 46.6 %copy-start.53 = (f32[2,16]{1,0:T(2,128)S(1)}, f32[2,16]{1,0:T(2,128)}, u32[]{:S(2)}) copy-start(f32[2,16]{1,0:T(2,128)} %param.23) | copy-start | bytes 388
  164.4 60.2 %copy-start.17 = (f32[4,128,16]{2,1,0:T(8,128)S(1)}, f32[4,128,16]{2,1,0:T(8,128)}, u32[]{:S(2)}) copy-start(f32[4,128,16]{2,1,0:T(8,128)} %copy-done.16) | copy-start | bytes 98308
  165.4 61.8 %copy-start.18 = (f32[4,128,16]{2,1,0:T(8,128)S(1)}, f32[4,128,16]{2,1,0:T(8,128)}, u32[]{:S(2)}) copy-start(f32[4,128,16]{2,1,0:T(8,128)} %get-tuple-element.144) | copy-start | bytes 98308
  165.4 69.4 %all-gather.19.cloned.1.call-start = ((), (), s32[]{:S(2)}) async-start(), calls=%async_computation.6 | async-start | bytes 1310720 | tf_op jit(solution)/shard_map/all_gather | solution.py:56
  174.1 37.4 %copy-start.33 = (f32[16]{0:T(128)}, f32[16]{0:T(128)S(1)}, u32[]{:S(2)}) copy-start(f32[16]{0:T(128)S(1)} %get-tuple-element.455) | copy-start | bytes 196
  184.8 76.0 %all-gather.15.cloned.1.call-start = ((), (), s32[]{:S(2)}) async-start(), calls=%async_computation.4 | async-start | bytes 1310720 | tf_op jit(solution)/shard_map/all_gather | solution.py:56
  191.8 32.8 %copy-start.34 = (f32[16]{0:T(128)}, f32[16]{0:T(128)S(1)}, u32[]{:S(2)}) copy-start(f32[16]{0:T(128)S(1)} %get-tuple-element.447) | copy-start | bytes 196
  191.8 32.8 %copy-start.36 = (f32[16]{0:T(128)}, f32[16]{0:T(128)S(1)}, u32[]{:S(2)}) copy-start(f32[16]{0:T(128)S(1)} %get-tuple-element.448) | copy-start | bytes 196
  191.8 32.8 %copy-start.38 = (f32[16]{0:T(128)}, f32[16]{0:T(128)S(1)}, u32[]{:S(2)}) copy-start(f32[16]{0:T(128)S(1)} %get-tuple-element.449) | copy-start | bytes 196
  192.5 26.7 %copy-start.31 = (f32[16]{0:T(128)}, f32[16]{0:T(128)S(1)}, u32[]{:S(2)}) copy-start(f32[16]{0:T(128)S(1)} %get-tuple-element.446) | copy-start | bytes 196
  239.9 20.9 %copy-start.9 = (bf16[32,64,128]{2,1,0:T(8,128)(2,1)S(1)}, bf16[32,64,128]{2,1,0:T(8,128)(2,1)}, u32[]{:S(2)}) copy-start(bf16[32,64,128]{2,1,0:T(8,128)(2,1)} %copy-done.8) | copy-start | bytes 1572868
  239.9 20.9 %copy-start.32 = (f32[16]{0:T(128)S(1)}, f32[16]{0:T(128)}, u32[]{:S(2)}) copy-start(f32[16]{0:T(128)} %copy-done.31) | copy-start | bytes 196
  239.9 20.9 %copy-start.35 = (f32[16]{0:T(128)S(1)}, f32[16]{0:T(128)}, u32[]{:S(2)}) copy-start(f32[16]{0:T(128)} %copy-done.34) | copy-start | bytes 196
  239.9 20.9 %copy-start.37 = (f32[16]{0:T(128)S(1)}, f32[16]{0:T(128)}, u32[]{:S(2)}) copy-start(f32[16]{0:T(128)} %copy-done.36) | copy-start | bytes 196
  239.9 20.9 %copy-start.39 = (f32[16]{0:T(128)S(1)}, f32[16]{0:T(128)}, u32[]{:S(2)}) copy-start(f32[16]{0:T(128)} %copy-done.38) | copy-start | bytes 196
  239.9 20.9 %copy-start.44 = (f32[16]{0:T(128)S(1)}, f32[16]{0:T(128)}, u32[]{:S(2)}) copy-start(f32[16]{0:T(128)} %copy-done.43) | copy-start | bytes 196
  239.9 20.9 %copy-start.46 = (f32[16]{0:T(128)S(1)}, f32[16]{0:T(128)}, u32[]{:S(2)}) copy-start(f32[16]{0:T(128)} %copy-done.45) | copy-start | bytes 196
  239.9 20.9 %copy-start.49 = (f32[16]{0:T(128)S(1)}, f32[16]{0:T(128)}, u32[]{:S(2)}) copy-start(f32[16]{0:T(128)} %get-tuple-element.413) | copy-start | bytes 196
  239.9 24.1 %copy-start.13 = (bf16[4,128,128]{1,0,2:T(4,128)(2,1)S(1)}, bf16[4,128,128]{1,0,2:T(4,128)(2,1)}, u32[]{:S(2)}) copy-start(bf16[4,128,128]{1,0,2:T(4,128)(2,1)} %copy-done.12) | copy-start | bytes 393220
  242.5 21.6 %copy-start.3 = (bf16[4,128,16,64]{1,0,3,2:T(4,128)(2,1)S(1)}, bf16[4,128,16,64]{1,0,3,2:T(4,128)(2,1)}, u32[]{:S(2)}) copy-start(bf16[4,128,16,64]{1,0,3,2:T(4,128)(2,1)} %copy-done.2) | copy-start | bytes 3145732
  242.5 21.6 %copy-start.50 = (f32[16]{0:T(128)S(1)}, f32[16]{0:T(128)}, u32[]{:S(2)}) copy-start(f32[16]{0:T(128)} %get-tuple-element.459) | copy-start | bytes 196
  285.2 33.2 %copy-start.1 = (bf16[2048,512]{1,0:T(8,128)(2,1)S(1)}, bf16[2048,512]{1,0:T(8,128)(2,1)}, u32[]{:S(2)}) copy-start(bf16[2048,512]{1,0:T(8,128)(2,1)} %param.18) | copy-start | bytes 6291460
  (33 other events, 233.0 us)
Sparse Core Ops, SparseCore 0:
  158.0 24.4 all-gather.16
  184.2 24.4 all-gather.12
  210.3 24.3 all-gather.18
  236.3 24.4 all-gather.14
where the time goes:
time: 327 us; the launch traced here: 325 us
  blocking collectives  87.7 us (27%)
  waiting for transfers between devices  76.9 us (24%)
  matrix products  57.6 us (18%)
  local copies, waits for them, and re-layouts  37.8 us (12%)
  other arithmetic  37 us (11%)
  between operations  14.7 us (4%)
  starting transfers between devices  12.9 us (4%)
    all_gather x4, waiting for transfers between devices, entering_2(): lax.all_gather(part.astype(kind), axis)  46.6 us
    all_gather x6, blocking collectives, entering_2(): lax.all_gather(part.astype(kind), axis)  41.4 us
    all_to_all x1, blocking collectives, summed_on_arrival(): lax.all_to_all(split_up(shard, dim, devices), axis, 0, 0, tiled=True)  30.2 us
    all_to_all x1, waiting for transfers between devices, sent_to_all(): lax.all_to_all(jnp.broadcast_to(shard[None], (devices, *shard.shape)), ax...  24.4 us
    dot_general x8, matrix products, advance(): jnp.einsum('hts,shp->thp', weights, x_block, preferred_element_type=jnp.f...  18.5 us
    dot_general x5, matrix products, per_device(): jnp.einsum('frd,dk->frk', shard_piece, matrix, preferred_element_type=jnp...  16.7 us
    all_to_all x1, blocking collectives, sent_to_all(): lax.all_to_all(jnp.broadcast_to(shard[None], (devices, *shard.shape)), ax...  11.6 us
    dot_general x8, matrix products, advance(): jnp.einsum('sn,shp->hpn', b_block, carried, preferred_element_type=jnp.fl...  9.55 us
  transfers between devices with their start and end apart: 7, of which 6 were waited for; matrix products, arithmetic and copies ran while one was open for 8% of the time, Pallas kernels for 0%

commit v1 on v0

v1 whole, which is shorter than its diff:
```python
import jax
import jax.numpy as jnp
from jax import lax
from jax.experimental import pallas as pl
from jax.experimental.pallas import tpu as pltpu
from jax.sharding import PartitionSpec as P

BF = jnp.bfloat16
F32 = jnp.float32
FRAMES = 32
TOK = 512
BLK = 128
NBLK = 4
CH = 1024
D = 2048
HALF = 256
HALO = 8
LOG2E = 1.4426950408889634
D_INNER = 4096
VM = pl.BlockSpec(memory_space=pltpu.VMEM)
ANY = pl.BlockSpec(memory_space=pl.ANY)
MSG = 72


def silu(x):
    return 0.5 * x * (1.0 + jnp.tanh(0.5 * x))


def dot(a, b):
    return jnp.dot(a, b, preferred_element_type=F32)


def dev(frame, row):
    return {"frame": frame, "row": row}


def place():
    frame, row = lax.axis_index("frame"), lax.axis_index("row")
    core = lax.rem(row, 2)
    return frame, row, core, lax.div(row, 2)


def remote(src, dst, send, recv, target):
    return pltpu.make_async_remote_copy(src, dst, send, recv, device_id=target)


CHUNKS = 4
CROWS = 128 // CHUNKS


def project_body(
    tok_ref, wg_ref, wv_ref, ws_ref, wt_ref,
    gate_ref, xr_ref, halo_ref, bc_ref, st_ref,
    tb, wg, wv, ws, wt, wc, w_sem, s_sem, r_sem,
):
    frame, row, core, hi = place()
    partner = row + 1 - 2 * core
    across = lax.rem(row + 2, 4)
    loads = []
    for i, (src, dst) in enumerate(((wv_ref, wv), (wg_ref, wg), (ws_ref, ws), (wt_ref, wt))):
        copy = pltpu.make_async_copy(src, dst, w_sem.at[i])
        copy.start()
        loads.append(copy)

    barrier = pltpu.get_barrier_semaphore()
    first, final = frame == 0, frame == FRAMES - 1
    for peer in (partner, across):
        pl.semaphore_signal(barrier, inc=1, device_id=dev(frame, peer))

    @pl.when(jnp.logical_not(first))
    def _():
        pl.semaphore_signal(barrier, inc=1, device_id=dev(frame - 1, 3))

    @pl.when(jnp.logical_not(final))
    def _():
        pl.semaphore_signal(barrier, inc=1, device_id=dev(frame + 1, 0))

    to_next = jnp.logical_and(row == 3, jnp.logical_not(final))
    to_prev = jnp.logical_and(row == 0, jnp.logical_not(first))
    pl.semaphore_wait(barrier, jnp.where(jnp.logical_or(to_next, to_prev), 6, 2))

    cross, local = [], []
    for i in range(CHUNKS):
        rows = pl.ds(i * CROWS, CROWS)
        copy = remote(
            tok_ref.at[rows],
            tb.at[pl.ds(HALF + 16 + core * 128 + i * CROWS, CROWS)],
            s_sem.at[i], r_sem.at[i], dev(frame, across),
        )
        copy.start()
        cross.append(copy)
    mine = remote(
        tok_ref, tb.at[pl.ds(core * 128, 128)], s_sem.at[CHUNKS], r_sem.at[CHUNKS],
        dev(frame, partner),
    )
    mine.start()

    def halo_copies(up):
        src = tok_ref.at[pl.ds(128 - HALO if up else 0, HALO)]
        dst = tb.at[pl.ds(HALF + (0 if up else HALO), HALO)]
        base = 2 * CHUNKS + 1 + (0 if up else 4)
        return [
            remote(
                src, dst, s_sem.at[base + r], r_sem.at[2 * CHUNKS + 1 + (0 if up else 1)],
                dev(frame + 1 if up else frame - 1, r),
            )
            for r in range(4)
        ]

    for up, flag in ((True, to_next), (False, to_prev)):

        @pl.when(flag)
        def _(up=up):
            for copy in halo_copies(up):
                copy.start()

    tb[pl.ds(core * 128, 128), :] = tok_ref[...]
    for up, flag in ((True, first), (False, final)):

        @pl.when(flag)
        def _(up=up):
            tb[pl.ds(HALF + (0 if up else HALO), HALO), :] = jnp.zeros((HALO, D), BF)

    def multiply(lo, count, put):
        def over(weight, columns, width, store):
            @pl.loop(0, columns // width)
            def _(n):
                cols = pl.ds(pl.multiple_of(n * width, width), width)
                out = dot(tb[lo : lo + count, :], weight[:, cols]).astype(BF)
                store(out, cols)

        return over

    def phase(lo, count, skip, base, waits):
        over = multiply(lo, count, None)
        rows = pl.ds(pl.multiple_of(base, HALF), HALF)

        def put(ref):
            def store(out, cols):
                ref[rows, cols] = out[skip:]

            return store

        def put_value(out, cols):
            xr_ref[rows, cols] = out[skip:]
            if skip:
                halo_ref[:, cols] = out[:skip]

        if waits:
            loads[0].wait()
        over(wv, CH, 256, put_value)
        if waits:
            loads[1].wait()
        over(wg, CH, 256, put(gate_ref))
        if waits:
            loads[2].wait()
            loads[3].wait()
            wc[...] = jnp.zeros_like(wc)
            wc[:, 0:16] = wt[0]
            wc[:, 16:32] = wt[1]
        over(ws, 512, 256, put(bc_ref))
        over(wc, 128, 128, put(st_ref))

    mine.wait_recv()
    phase(0, HALF, 0, hi * HALF, True)

    for i in range(CHUNKS):
        cross[i].wait_recv()
        rows = pl.ds(HALF + 16 + core * 128 + i * CROWS, CROWS)
        copy = remote(
            tb.at[rows], tb.at[rows], s_sem.at[CHUNKS + 1 + i], r_sem.at[CHUNKS + 1 + i],
            dev(frame, partner),
        )
        copy.start()
        local.append(copy)
    for up, flag in ((True, first), (False, final)):

        @pl.when(jnp.logical_not(flag))
        def _(up=up):
            halo_copies(up)[0].wait_recv()

    for copy in local:
        copy.wait_recv()
    phase(HALF, HALF + 16, 16, (1 - hi) * HALF, False)
    mine.wait_send()
    for copy in cross + local:
        copy.wait_send()
    for up, flag in ((True, to_next), (False, to_prev)):

        @pl.when(flag)
        def _(up=up):
            for copy in halo_copies(up):
                copy.wait_send()


def project(tokens, w_gate, w_value, w_state, w_step):
    sds = jax.ShapeDtypeStruct
    return pl.pallas_call(
        project_body,
        name="project",
        out_shape=(
            sds((TOK, CH), BF), sds((TOK, CH), BF), sds((16, CH), BF),
            sds((TOK, 512), BF), sds((TOK, 128), BF),
        ),
        in_specs=[VM, ANY, ANY, ANY, ANY],
        out_specs=(VM,) * 5,
        scratch_shapes=[
            pltpu.VMEM((HALF + 16 + HALF, D), BF),
            pltpu.VMEM((D, CH), BF), pltpu.VMEM((D, CH), BF), pltpu.VMEM((D, 512), BF),
            pltpu.VMEM((2, D, 16), BF), pltpu.VMEM((D, 128), BF),
            pltpu.SemaphoreType.DMA((4,)),
            pltpu.SemaphoreType.DMA((2 * CHUNKS + 1 + 8,)),
            pltpu.SemaphoreType.DMA((2 * CHUNKS + 3,)),
        ],
        compiler_params=pltpu.CompilerParams(
            collective_id=0, has_side_effects=True, vmem_limit_bytes=60 * 1024 * 1024
        ),
    )(tokens, w_gate, w_value, w_state, w_step)


def expand(values, base):
    lane = lax.broadcasted_iota(jnp.int32, (1, 128), 1)
    return jnp.where(lane < 64, values[:, base : base + 1], values[:, base + 1 : base + 2])


def lanes(group):
    return slice(group * 128, group * 128 + 128)


def scan_body(
    xr_ref, halo_ref, bc_ref, st_ref, par_ref, taps_ref,
    msg_ref, y_ref, ef_ref,
    xp, xs, xdt, start, state, car, cum_s, dt_s, tot_s,
):
    row_i = lax.broadcasted_iota(jnp.int32, (BLK, BLK), 0)
    col_i = lax.broadcasted_iota(jnp.int32, (BLK, BLK), 1)
    lower = (row_i >= col_i)
    forward = col_i < 16
    xp[0:8, :] = halo_ref[0:8, :].astype(F32)
    xp[8 : 8 + TOK, :] = xr_ref[...].astype(F32)
    xp[8 + TOK :, :] = halo_ref[8:16, :].astype(F32)
    bias, rate = par_ref[0:1, :], par_ref[1:2, :] * LOG2E
    raw = st_ref[...].astype(F32) + bias
    dt = jnp.maximum(raw, 0.0) + jnp.log1p(jnp.exp(-jnp.abs(raw)))
    dt_s[...] = dt
    step = -dt * rate
    tri = lower.astype(BF)
    totals = []
    for j in range(NBLK):
        part = step[j * BLK : (j + 1) * BLK]
        high = part.astype(BF)
        rest = part - high.astype(F32)
        mid = rest.astype(BF)
        low = (rest - mid.astype(F32)).astype(BF)
        cum = dot(tri, high) + (dot(tri, mid) + dot(tri, low))
        total = cum[BLK - 1 : BLK]
        cum_s[j * BLK : (j + 1) * BLK] = jnp.where(forward, cum, (total - cum) + part)
        totals.append(total)
    zero = jnp.zeros((1, 128), F32)
    before, after = [zero], [zero]
    for j in range(NBLK - 1):
        before.append(before[-1] + totals[j])
        after.append(after[-1] + totals[NBLK - 1 - j])
    after = after[::-1]
    forward1 = forward[0:1]
    for j in range(NBLK):
        rows = slice(j * BLK, (j + 1) * BLK)
        ef_ref[rows] = jnp.exp2(cum_s[rows] + jnp.where(forward1, before[j], after[j]))
        tot_s[j : j + 1] = totals[j]
    whole = before[-1] + totals[-1]

    @pl.loop(0, NBLK)
    def _(j):
        for g in range(8):
            window = xp[pl.ds(pl.multiple_of(j * BLK, BLK), BLK + 16), lanes(g)]
            shifted = {
                o: pltpu.roll(window, (-o) % (BLK + 16), 0)[8 : 8 + BLK] for o in range(-3, 4)
            }
            for d in range(2):
                acc = None
                for k in range(4):
                    term = taps_ref[d, k : k + 1, lanes(g)] * shifted[3 - k if d else k - 3]
                    acc = term if acc is None else acc + term
                xs[d, pl.ds(pl.multiple_of(j * BLK, BLK), BLK), lanes(g)] = silu(acc).astype(BF)

    state[...] = jnp.zeros_like(state)

    @pl.loop(0, NBLK)
    def _(i):
        for d in range(2):
            j = i if d == 0 else NBLK - 1 - i
            rows = pl.ds(pl.multiple_of(j * BLK, BLK), BLK)
            total = tot_s[pl.ds(j, 1)]
            dt_j = dt_s[rows]
            fade = jnp.exp2(total - cum_s[rows]) * dt_j
            kept = jnp.exp2(total)
            for g in range(8):
                x = xs[d, rows, lanes(g)].astype(F32)
                car[:, lanes(g)] = (x * expand(fade, d * 16 + 2 * g)).astype(BF)
                xdt[d, rows, lanes(g)] = (x * expand(dt_j, d * 16 + 2 * g)).astype(BF)
            b = bc_ref[rows, d * 256 : d * 256 + 128]
            bt = b.astype(F32).T.astype(BF)
            for g in range(8):
                old = state[d, :, lanes(g)]
                start[d, pl.ds(j, 1), :, lanes(g)] = old.astype(BF)[None]
                state[d, :, lanes(g)] = (
                    old * expand(kept, d * 16 + 2 * g) + dot(bt, car[:, lanes(g)])
                )

    row8 = lax.broadcasted_iota(jnp.int32, (8, 128), 0)
    shrink = jnp.exp2(whole)
    for g in range(8):
        decay = [expand(shrink, d * 16 + 2 * g) for d in range(2)]
        high = [v.astype(BF).astype(F32) for v in decay]
        tail = jnp.zeros((8, 128), F32)
        for k, v in enumerate((high[0], decay[0] - high[0], high[1], decay[1] - high[1])):
            tail = jnp.where(row8 == k, v, tail)
        for r in range(4):
            piece = g * 4 + r
            for d in range(2):
                msg_ref[piece, d * 32 : d * 32 + 32] = state[
                    d, r * 32 : r * 32 + 32, lanes(g)
                ].astype(BF)
            msg_ref[piece, 64:72] = tail.astype(BF)

    skip = par_ref[2:3, :]
    upper = col_i >= row_i

    @pl.loop(0, NBLK)
    def _(j):
        rows = pl.ds(pl.multiple_of(j * BLK, BLK), BLK)
        cum = cum_s[rows]
        cum_t = cum.T
        grown = jnp.exp2(cum)
        c, scores = [], []
        for d in range(2):
            b = bc_ref[rows, d * 256 : d * 256 + 128]
            c.append(bc_ref[rows, d * 256 + 128 : d * 256 + 256])
            s = lax.dot_general(
                c[d], b, (((1,), (1,)), ((), ())), preferred_element_type=F32
            )
            scores.append(jnp.where(lower if d == 0 else upper, s, 0.0))
        for g in range(8):
            values = jnp.concatenate([xdt[0, rows, lanes(g)], xdt[1, rows, lanes(g)]], axis=0)
            outs = []
            for k in range(2):
                h = 2 * g + k
                w = []
                for d in range(2):
                    n = d * 16 + h
                    gap = jnp.minimum(cum[:, n : n + 1] - cum_t[n : n + 1, :], 0.0)
                    w.append((scores[d] * jnp.exp2(gap)).astype(BF))
                outs.append(dot(jnp.concatenate(w, axis=1), values))
            y = jnp.where(col_i < 64, outs[0], outs[1])
            for d in range(2):
                carried = dot(c[d], start[d, j, :, lanes(g)])
                y = y + expand(grown, d * 16 + 2 * g) * carried
                y = y + expand(skip, d * 16 + 2 * g) * xs[d, rows, lanes(g)].astype(F32)
            y_ref[rows, lanes(g)] = y


def local_scan(x_raw, halo, bc, step, params, taps):
    sds = jax.ShapeDtypeStruct
    return pl.pallas_call(
        scan_body,
        name="local_scan",
        out_shape=(sds((32, MSG, 128), BF), sds((TOK, CH), F32), sds((TOK, 128), F32)),
        in_specs=[VM] * 6,
        out_specs=(VM,) * 3,
        scratch_shapes=[
            pltpu.VMEM((TOK + 16, CH), F32),
            pltpu.VMEM((2, TOK, CH), BF),
            pltpu.VMEM((2, TOK, CH), BF),
            pltpu.VMEM((2, NBLK, 128, CH), BF),
            pltpu.VMEM((2, 128, CH), F32),
            pltpu.VMEM((BLK, CH), BF),
            pltpu.VMEM((TOK, 128), F32),
            pltpu.VMEM((TOK, 128), F32),
            pltpu.VMEM((8, 128), F32),
        ],
        compiler_params=pltpu.CompilerParams(vmem_limit_bytes=60 * 1024 * 1024),
    )(x_raw, halo, bc, step, params, taps)


def states_body(msg_ref, inc_ref, got, out, back, s_sem, r_sem, s2_sem, r2_sem):
    frame, row, core, hi = place()
    barrier = pltpu.get_barrier_semaphore()
    peers = [lax.rem(frame + i, FRAMES) for i in range(1, FRAMES)]
    for peer in peers:
        pl.semaphore_signal(barrier, inc=1, device_id=dev(peer, row))
    pl.semaphore_wait(barrier, FRAMES - 1)
    copies = []
    for i, peer in enumerate(peers):
        copy = remote(msg_ref.at[peer], got.at[frame], s_sem.at[i], r_sem.at[i], dev(peer, row))
        copy.start()
        copies.append(copy)
    got[frame] = msg_ref[frame]
    for copy in copies:
        copy.wait_recv()
    for d in range(2):
        state = jnp.zeros((32, 128), F32)
        for g in range(FRAMES) if d == 0 else reversed(range(FRAMES)):
            out[g, d * 32 : d * 32 + 32] = state.astype(BF)
            tail = got[g, 64:72].astype(F32)
            decay = tail[2 * d : 2 * d + 1] + tail[2 * d + 1 : 2 * d + 2]
            state = decay * state + got[g, d * 32 : d * 32 + 32].astype(F32)
    returns = []
    for i, peer in enumerate(peers):
        copy = remote(out.at[peer], back.at[frame], s2_sem.at[i], r2_sem.at[i], dev(peer, row))
        copy.start()
        returns.append(copy)
    back[frame] = out[frame]
    for copy in returns:
        copy.wait_recv()
    inc_ref[...] = back[...]
    for copy in copies + returns:
        copy.wait_send()


def exchange(msg):
    return pl.pallas_call(
        states_body,
        name="states",
        out_shape=jax.ShapeDtypeStruct((32, 64, 128), BF),
        in_specs=[VM],
        out_specs=VM,
        scratch_shapes=[
            pltpu.VMEM((32, MSG, 128), BF),
            pltpu.VMEM((32, 64, 128), BF),
            pltpu.VMEM((32, 64, 128), BF),
        ]
        + [pltpu.SemaphoreType.DMA((31,))] * 4,
        compiler_params=pltpu.CompilerParams(collective_id=1, has_side_effects=True),
    )(msg)


COLS = 512
NCOL = D // COLS


def finish_body(
    y_ref, gate_ref, bc_ref, ef_ref, inc_ref, gain_ref, w_ref,
    out_ref,
    w, inc, normed, sq, to_partner, from_partner, to_across, from_across, own,
    sq_out, sq_part, sq_cross, sq_far,
    w_sem, s_sem, r_sem,
):
    frame, row, core, hi = place()
    partner = row + 1 - 2 * core
    across = lax.rem(row + 2, 4)
    corner = lax.rem(partner + 2, 4)
    load = pltpu.make_async_copy(w_ref, w, w_sem)
    load.start()
    barrier = pltpu.get_barrier_semaphore()
    for peer in (partner, across):
        pl.semaphore_signal(barrier, inc=1, device_id=dev(frame, peer))
    for g in range(8):
        for r in range(4):
            for d in range(2):
                inc[d, r * 32 : r * 32 + 32, lanes(g)] = inc_ref[
                    g * 4 + r, d * 32 : d * 32 + 32
                ]

    order = (corner, across, partner, row)

    @pl.loop(0, 4)
    def _(n):
        target = jnp.where(
            n == 0, corner, jnp.where(n == 1, across, jnp.where(n == 2, partner, row))
        )
        rows = pl.ds(pl.multiple_of(target * BLK, BLK), BLK)
        ef = ef_ref[rows]
        total = jnp.zeros((BLK, 1), F32)
        for g in range(8):
            y = y_ref[rows, lanes(g)]
            for d in range(2):
                c = bc_ref[rows, d * 256 + 128 : d * 256 + 256]
                y = y + expand(ef, d * 16 + 2 * g) * dot(c, inc[d, :, lanes(g)])
            gated = y * silu(gate_ref[rows, lanes(g)].astype(F32))
            total = total + jnp.sum(gated * gated, axis=1, keepdims=True)
            normed[pl.ds(pl.multiple_of(n * BLK, BLK), BLK), lanes(g)] = (
                gated * gain_ref[:, lanes(g)]
            ).astype(BF)
        sq[n] = jnp.broadcast_to(total, (BLK, BLK)).T[0:8]

    load.wait()
    pl.semaphore_wait(barrier, 2)
    sq_out[0] = sq[0]
    sq_out[1] = sq[2]
    sq_copy = remote(sq_out, sq_part, s_sem.at[0], r_sem.at[0], dev(frame, partner))
    sq_copy.start()
    first, second, third = [], [], []
    for k in range(NCOL):
        cols = slice(k * COLS, (k + 1) * COLS)
        part = dot(normed[0:HALF, :], w[:, cols])
        to_partner[0, k] = part[0:BLK].astype(BF)
        copy = remote(
            to_partner.at[0, k], from_partner.at[0, k], s_sem.at[1 + k], r_sem.at[1 + k],
            dev(frame, partner),
        )
        copy.start()
        first.append(copy)
        own[k] = part[BLK:]

    sq_copy.wait_recv()
    sq_cross[...] = sq[1] + sq_part[0]
    far_copy = remote(sq_cross, sq_far, s_sem.at[1 + NCOL], r_sem.at[1 + NCOL], dev(frame, across))
    far_copy.start()
    for k in range(NCOL):
        first[k].wait_recv()
        to_across[k] = (own[k] + from_partner[0, k].astype(F32)).astype(BF)
        copy = remote(
            to_across.at[k], from_across.at[k], s_sem.at[2 + NCOL + k], r_sem.at[2 + NCOL + k],
            dev(frame, across),
        )
        copy.start()
        second.append(copy)
    for k in range(NCOL):
        cols = slice(k * COLS, (k + 1) * COLS)
        part = dot(normed[HALF:, :], w[:, cols])
        to_partner[1, k] = part[0:BLK].astype(BF)
        copy = remote(
            to_partner.at[1, k], from_partner.at[1, k],
            s_sem.at[2 + 2 * NCOL + k], r_sem.at[2 + 2 * NCOL + k],
            dev(frame, partner),
        )
        copy.start()
        third.append(copy)
        own[k] = part[BLK:]
    far_copy.wait_recv()
    mean = (sq[3] + sq_part[1] + sq_far[...]) * (1.0 / D_INNER)
    scale = jnp.broadcast_to(lax.rsqrt(mean + 1e-05)[0:1], (BLK, BLK)).T[:, 0:1]
    for k in range(NCOL):
        third[k].wait_recv()
        own[k] = own[k] + from_partner[1, k].astype(F32)
    for k in range(NCOL):
        cols = slice(k * COLS, (k + 1) * COLS)
        second[k].wait_recv()
        out_ref[:, cols] = (scale * (own[k] + from_across[k].astype(F32))).astype(BF)
    for copy in [sq_copy, far_copy] + first + second + third:
        copy.wait_send()


def finish(y, gate, bc, ef, inc, gain, w_out):
    return pl.pallas_call(
        finish_body,
        name="finish",
        out_shape=jax.ShapeDtypeStruct((BLK, D), BF),
        in_specs=[VM] * 6 + [ANY],
        out_specs=VM,
        scratch_shapes=[
            pltpu.VMEM((CH, D), BF),
            pltpu.VMEM((2, 128, CH), BF),
            pltpu.VMEM((TOK, CH), BF),
            pltpu.VMEM((4, 8, 128), F32),
            pltpu.VMEM((2, NCOL, BLK, COLS), BF),
            pltpu.VMEM((2, NCOL, BLK, COLS), BF),
            pltpu.VMEM((NCOL, BLK, COLS), BF),
            pltpu.VMEM((NCOL, BLK, COLS), BF),
            pltpu.VMEM((NCOL, BLK, COLS), F32),
            pltpu.VMEM((2, 8, 128), F32),
            pltpu.VMEM((2, 8, 128), F32),
            pltpu.VMEM((8, 128), F32),
            pltpu.VMEM((8, 128), F32),
            pltpu.SemaphoreType.DMA,
            pltpu.SemaphoreType.DMA((2 + 3 * NCOL,)),
            pltpu.SemaphoreType.DMA((2 + 3 * NCOL,)),
        ],
        compiler_params=pltpu.CompilerParams(
            collective_id=2, has_side_effects=True, vmem_limit_bytes=60 * 1024 * 1024
        ),
    )(y, gate, bc, ef, inc, gain, w_out)


def per_device(
    tokens, w_gate, w_value, w_state_proj, w_step, step_bias, decay_rate, conv_taps,
    skip_gain, norm_gain, w_out,
):
    params = jnp.stack([step_bias.reshape(32), decay_rate.reshape(32), skip_gain.reshape(32)])
    params = jnp.pad(params, ((0, 5), (0, 96)))
    gate, x_raw, halo, bc, step = project(tokens[0], w_gate, w_value, w_state_proj, w_step)
    msg, y, ef = local_scan(x_raw, halo, bc, step, params, conv_taps)
    inc = exchange(msg)
    out = finish(y, gate, bc, ef, inc, norm_gain[None, :], w_out)
    return out[None]


def solution(mesh):
    in_specs = (
        P("frame", "row", None), P(None, "row"), P(None, "row"), P(), P(None, None, "row"),
        P(None, "row"), P(None, "row"), P(None, None, "row"), P(None, "row"), P("row"),
        P("row", None),
    )
    return jax.shard_map(
        per_device, mesh=mesh, in_specs=in_specs, out_specs=P("frame", "row", None),
        check_vma=False,
    )
```

time: 327 us -> 107 us (0.33)
  Pallas kernels: 0 us -> 99.9 us
  blocking collectives: 87.7 us -> 0 us
  waiting for transfers between devices: 76.9 us -> 0 us
  matrix products: 57.6 us -> 0 us
  other arithmetic: 37 us -> 0.6 us
  local copies, waits for them, and re-layouts: 37.8 us -> 6.38 us
  between operations: 14.7 us -> 0.03 us
  starting transfers between devices: 12.9 us -> 0 us
    pallas_call x0 -> x4, Pallas kernels: none -> 99.9 us  [the longest x1 27.5 us: exchange(): pl.pallas_call(states_body, name='states', out_shape=jax.ShapeDtypeStruct...]
    dot_general x32 -> x0, matrix products: 57.6 us -> none  [the longest x8 18.5 us: advance(): jnp.einsum('hts,shp->thp', weights, x_block, preferred_element_type=jnp.f...]
    all_gather x4 -> x0, waiting for transfers between devices: 46.6 us -> none  [entering_2(): lax.all_gather(part.astype(kind), axis)]
    all_to_all x2 -> x0, blocking collectives: 41.8 us -> none  [the longest x1 30.2 us: summed_on_arrival(): lax.all_to_all(split_up(shard, dim, devices), axis, 0, 0, tiled=True)]
    all_gather x6 -> x0, blocking collectives: 41.4 us -> none  [entering_2(): lax.all_gather(part.astype(kind), axis)]
    all_to_all x1 -> x0, waiting for transfers between devices: 24.4 us -> none  [sent_to_all(): lax.all_to_all(jnp.broadcast_to(shard[None], (devices, *shard.shape)), ax...]
    convert_element_type x10 -> x0, other arithmetic: 14.5 us -> none  [the longest x8 7.07 us: entering_2(): part.astype(kind)]
    dynamic_update_slice x8 -> x0, other arithmetic: 6.96 us -> none  [local_pass(): lax.scan(advance, (state_zero, jnp.zeros((heads_here,), jnp.float32)), bl...]
  transfers between devices with their start and end apart: 7 -> 0, of which waited for: 6 -> 0; matrix products, arithmetic and copies ran while one was open for 8% -> 0% of each run, Pallas kernels for 0% -> 0%
where the time goes in v1:
time: 107 us
  Pallas kernels  99.9 us (93%)
  local copies, waits for them, and re-layouts  6.38 us (6%)
    pallas_call x1, Pallas kernels, exchange(): pl.pallas_call(states_body, name='states', out_shape=jax.ShapeDtypeStruct...  27.5 us
    pallas_call x1, Pallas kernels, project(): pl.pallas_call(project_body, name='project', out_shape=(sds((TOK, CH), BF...  26.9 us
    pallas_call x1, Pallas kernels, finish(): pl.pallas_call(finish_body, name='finish', out_shape=jax.ShapeDtypeStruct...  26.7 us
    pallas_call x1, Pallas kernels, local_scan(): pl.pallas_call(scan_body, name='local_scan', out_shape=(sds((32, MSG, 128...  18.9 us
    unnamed x2, local copies, waits for them, and re-layouts  4.11 us
    another operation x3, local copies, waits for them, and re-layouts, per_device(): jnp.stack([step_bias.reshape(32), decay_rate.reshape(32), skip_gain.resha...  2.28 us

profile of v1, /device:TPU:1, one launch (start us, length us, event | category | flops | bytes accessed | tf_op | source)
XLA Modules:
  0.0 106.9 jit_solution(17274411685714197834)
XLA Ops:
  0.0 0.8 stack_reshape.9
  0.8 0.8 stack_reshape.10
  1.5 0.8 stack_reshape.11
  2.3 0.6 select_maximum_fusion.par_ref
  2.9 2.2 %copy.12.wt_ref = bf16[2,2048,16]{2,1,0:T(8,128)(2,1)} copy(bf16[2,2048,16]{1,2,0:T(8,128)(2,1)} %param.15) | data formatting | bytes 262144 | tf_op args[4]
  5.1 26.9 %project.1 = (bf16[512,1024]{1,0:T(8,128)(2,1)}, bf16[512,1024]{1,0:T(8,128)(2,1)}, bf16[16,1024]{1,0:T(8,128)(2,1)}, bf16[512,512]{1,0:T(8,128)(2,1)}, bf16[512,128]{1,0:T(8,128)(2,1)}) custom-call(bf16[128,2048]{1,0:T(8,128)(2,1)} %bitcast.4, bf16[2048,1024]{1,0:T(8,128)(2,1)} %wg_ref.1, bf16[2048,1024]{1,0:T(8,128)(2,1)} %wv_ref.1, ...), custom_call_target="tpu_custom_call" | custom-call | tf_op jit(solution)/shard_map/project/pallas_call | solution.py:198
  32.0 18.9 %local_scan.1 = (bf16[32,72,128]{2,1,0:T(8,128)(2,1)}, f32[512,1024]{1,0:T(8,128)}, f32[512,128]{1,0:T(8,128)}) custom-call(bf16[512,1024]{1,0:T(8,128)(2,1)} %get-tuple-element.13.xr_ref, bf16[16,1024]{1,0:T(8,128)(2,1)} %get-tuple-element.14.halo_ref, bf16[512,512]{1,0:T(8,128)(2,1)} %get-tuple-element.15.bc_ref, ...), custom_call_target="tpu_custom_call" | custom-call | tf_op jit(solution)/shard_map/local_scan/pallas_call | solution.py:364
  50.8 27.5 %states.1.inc_ref = bf16[32,64,128]{2,1,0:T(8,128)(2,1)} custom-call(bf16[32,72,128]{2,1,0:T(8,128)(2,1)} %get-tuple-element.20.msg_ref), custom_call_target="tpu_custom_call" | custom-call | tf_op jit(solution)/shard_map/states/pallas_call | solution.py:421
  78.3 26.7 %finish.1 = bf16[128,2048]{1,0:T(8,128)(2,1)} custom-call(f32[512,1024]{1,0:T(8,128)} %get-tuple-element.17.y_ref, bf16[512,1024]{1,0:T(8,128)(2,1)} %get-tuple-element.18.gate_ref, bf16[512,512]{1,0:T(8,128)(2,1)} %get-tuple-element.15.bc_ref, f32[512,128]{1,0:T(8,128)} %get-tuple-element.19.ef_ref, bf16[32,64,128]{2,1,0:T(8,128)(2,1)} %states.1.inc_ref, ...), custom_call_target="tpu_custom_call" | custom-call | tf_op jit(solution)/shard_map/finish/pallas_call | solution.py:545
  105.1 1.9 %copy.14 = bf16[1,128,2048]{2,1,0:T(8,128)(2,1)} copy(bf16[1,128,2048]{2,1,0:T(8,128)(2,1)} %bitcast.3) | data formatting | bytes 1048576

commit v2 on v0

v2 whole, which is shorter than its diff:
```python
import jax
import jax.numpy as jnp
from jax import lax
from jax.experimental import pallas as pl
from jax.experimental.pallas import tpu as pltpu
from jax.sharding import PartitionSpec as P

BF = jnp.bfloat16
F32 = jnp.float32
FRAMES = 32
TOK = 512
BLK = 128
NBLK = 4
CH = 1024
D = 2048
HALF = 256
HALO = 8
LOG2E = 1.4426950408889634
D_INNER = 4096
VM = pl.BlockSpec(memory_space=pltpu.VMEM)
ANY = pl.BlockSpec(memory_space=pl.ANY)
MSG = 72


def silu(x):
    return 0.5 * x * (1.0 + jnp.tanh(0.5 * x))


def dot(a, b):
    return jnp.dot(a, b, preferred_element_type=F32)


def dev(frame, row):
    return {"frame": frame, "row": row}


def place():
    frame, row = lax.axis_index("frame"), lax.axis_index("row")
    core = lax.rem(row, 2)
    return frame, row, core, lax.div(row, 2)


def remote(src, dst, send, recv, target):
    return pltpu.make_async_remote_copy(src, dst, send, recv, device_id=target)


CHUNKS = 4
CROWS = 128 // CHUNKS
EDGE = 16
COLS = 512
NCOL = D // COLS
PEERS = FRAMES - 1


def expand(values, base):
    lane = lax.broadcasted_iota(jnp.int32, (1, 128), 1)
    return jnp.where(lane < 64, values[:, base : base + 1], values[:, base + 1 : base + 2])


def lanes(group):
    return slice(group * 128, group * 128 + 128)


def block(j, count=BLK, shift=0):
    return pl.ds(pl.multiple_of(j * BLK + shift, 16), count)


def layer_body(
    tok_ref, wg_ref, wv_ref, ws_ref, wt_ref, wo_ref,
    bias_ref, rate_ref, skip_ref, taps_ref, gain_ref,
    out_ref,
    tb, edge, wg, wv, ws, wt, wo, par, gate, bc,
    xp, xs, xdt, start, upd, car, cum_s, dt_s, tot_s, y_s, ef_s,
    msg, got, ret, inc, inc_m,
    normed, sq, to_partner, from_partner, to_across, from_across, own,
    sq_out, sq_part, sq_cross, sq_far,
    w_sem, g_s, g_r, a_s, a_r, b_s, b_r, f_s, f_r,
):
    frame, row, core, hi = place()
    partner = row + 1 - 2 * core
    across = lax.rem(row + 2, 4)
    corner = lax.rem(partner + 2, 4)
    peers = [lax.rem(frame + i, FRAMES) for i in range(1, FRAMES)]
    first, final = frame == 0, frame == FRAMES - 1

    mine = pl.ds(pl.multiple_of(EDGE + row * BLK, 16), BLK)
    loads = []
    for i, (src, dst) in enumerate((
        (tok_ref, tb.at[mine]), (wv_ref, wv), (ws_ref, ws),
        (wt_ref.at[0], wt.at[0:16]), (wt_ref.at[1], wt.at[16:32]),
        (wg_ref, wg), (wo_ref, wo),
    )):
        copy = pltpu.make_async_copy(src, dst, w_sem.at[i])
        copy.start()
        loads.append(copy)
    tb[0:EDGE, :] = jnp.zeros((EDGE, D), BF)
    tb[EDGE + TOK :, :] = jnp.zeros((EDGE, D), BF)
    barrier = pltpu.get_barrier_semaphore()
    for peer in (partner, across):
        pl.semaphore_signal(barrier, inc=1, device_id=dev(frame, peer))
    for peer in peers:
        pl.semaphore_signal(barrier, inc=1, device_id=dev(peer, row))

    @pl.when(jnp.logical_not(first))
    def _():
        pl.semaphore_signal(barrier, inc=1, device_id=dev(frame - 1, 3))

    @pl.when(jnp.logical_not(final))
    def _():
        pl.semaphore_signal(barrier, inc=1, device_id=dev(frame + 1, 0))

    to_next = jnp.logical_and(row == 3, jnp.logical_not(final))
    to_prev = jnp.logical_and(row == 0, jnp.logical_not(first))
    wt[32:128, :] = jnp.zeros((96, D), BF)
    par[...] = jnp.zeros_like(par)
    for i, ref in enumerate((bias_ref, rate_ref, skip_ref)):
        for d in range(2):
            par[i : i + 1, d * 16 : d * 16 + 16] = ref[d : d + 1, :]
    loads[0].wait()
    pl.semaphore_wait(
        barrier, 2 + PEERS + jnp.where(jnp.logical_or(to_next, to_prev), 4, 0)
    )

    def chunk_rows(owner, i, sender_hi):
        at = jnp.where(sender_hi == 1, i, CHUNKS - 1 - i) * CROWS
        return pl.ds(pl.multiple_of(EDGE + owner * BLK + at, 16), CROWS)

    def cross(i, owner, sender_hi):
        rows = chunk_rows(owner, i, sender_hi)
        return remote(tb.at[rows], tb.at[rows], g_s.at[i], g_r.at[i], dev(frame, across))

    def forward(i):
        rows = chunk_rows(across, i, 1 - hi)
        return remote(
            tb.at[rows], tb.at[rows], g_s.at[CHUNKS + i], g_r.at[CHUNKS + i], dev(frame, partner)
        )

    def forwarded(i):
        rows = chunk_rows(corner, i, 1 - hi)
        return remote(
            tb.at[rows], tb.at[rows], g_s.at[CHUNKS + i], g_r.at[CHUNKS + i], dev(frame, partner)
        )

    def pass_on(i):
        cross(i, across, 1 - hi).wait_recv()
        forward(i).start()

    near = remote(
        tb.at[mine], tb.at[mine], g_s.at[2 * CHUNKS], g_r.at[2 * CHUNKS], dev(frame, partner)
    )

    def halo_copies(up):
        src = tb.at[pl.ds(pl.multiple_of(EDGE + row * BLK + (BLK - HALO if up else 0), HALO), HALO)]
        dst = tb.at[pl.ds(EDGE - HALO if up else EDGE + TOK, HALO)]
        base = 2 * CHUNKS + 1 + (0 if up else 4)
        return [
            remote(
                src, dst, g_s.at[base + r], g_r.at[2 * CHUNKS + 1 + (0 if up else 1)],
                dev(frame + 1 if up else frame - 1, r),
            )
            for r in range(4)
        ]

    near.start()
    cross(0, row, hi).start()
    for up, flag in ((True, to_next), (False, to_prev)):

        @pl.when(flag)
        def _(up=up):
            for copy in halo_copies(up):
                copy.start()

    for i in range(1, CHUNKS):
        cross(i, row, hi).start()

    def over(read, weight, columns, width, store):
        @pl.loop(0, columns // width)
        def _(n):
            cols = pl.ds(pl.multiple_of(n * width, width), width)
            store(dot(read(), weight[:, cols]), cols)

    def phase(half, waits):
        def read():
            return tb[pl.ds(pl.multiple_of(EDGE + half * HALF, 16), HALF), :]

        rows = pl.ds(pl.multiple_of(half * HALF, 16), HALF)
        rows_x = pl.ds(pl.multiple_of(EDGE + half * HALF, 16), HALF)

        def put_x(out, cols):
            xp[rows_x, cols] = out.astype(BF).astype(F32)

        def put_bc(out, cols):
            bc[rows, cols] = out.astype(BF)

        if waits:
            loads[1].wait()
        over(read, wv, CH, 256, put_x)
        if waits:
            loads[2].wait()
        over(read, ws, 512, 256, put_bc)
        if waits:
            loads[3].wait()
            loads[4].wait()
        raw = lax.dot_general(
            read(), wt[...], (((1,), (1,)), ((), ())), preferred_element_type=F32
        ).astype(BF).astype(F32) + par[0:1, :]
        dt_s[rows, :] = jnp.maximum(raw, 0.0) + jnp.log1p(jnp.exp(-jnp.abs(raw)))

    row_i = lax.broadcasted_iota(jnp.int32, (BLK, BLK), 0)
    col_i = lax.broadcasted_iota(jnp.int32, (BLK, BLK), 1)
    lower, upper = row_i >= col_i, col_i >= row_i
    fwd_lane = col_i < 16

    def prepare(j):
        rows = block(j)
        part = dt_s[rows, :] * (par[1:2, :] * -LOG2E)
        high = part.astype(BF)
        rest = part - high.astype(F32)
        mid = rest.astype(BF)
        low = (rest - mid.astype(F32)).astype(BF)
        tri = lower.astype(BF)
        cum = dot(tri, high) + (dot(tri, mid) + dot(tri, low))
        total = cum[BLK - 1 : BLK]
        cum_s[rows, :] = jnp.where(fwd_lane, cum, (total - cum) + part)
        tot_s[pl.ds(j, 1), :] = total

    def convolve(j):
        for g in range(8):
            window = xp[block(j, BLK + 2 * EDGE), lanes(g)]
            size = BLK + 2 * EDGE
            shifted = {
                o: pltpu.roll(window, (-o) % size, 0)[EDGE : EDGE + BLK] if o
                else window[EDGE : EDGE + BLK]
                for o in range(-3, 4)
            }
            for d in range(2):
                acc = None
                for k in range(4):
                    term = taps_ref[d, k : k + 1, lanes(g)] * shifted[3 - k if d else k - 3]
                    acc = term if acc is None else acc + term
                xs[d, block(j), lanes(g)] = silu(acc).astype(BF)

    def update(j):
        rows = block(j)
        total = tot_s[pl.ds(j, 1), :]
        dt_j = dt_s[rows, :]
        fade = jnp.exp2(total - cum_s[rows, :]) * dt_j
        for d in range(2):
            b = bc[rows, d * 256 : d * 256 + 128]
            bt = b.astype(F32).T.astype(BF)
            for g in range(8):
                x = xs[d, rows, lanes(g)].astype(F32)
                xdt[d, rows, lanes(g)] = (x * expand(dt_j, d * 16 + 2 * g)).astype(BF)
                carried = (x * expand(fade, d * 16 + 2 * g)).astype(BF)
                upd[d, pl.ds(j, 1), :, lanes(g)] = dot(bt, carried)[None]

    def intra(j):
        rows = block(j)
        cum = cum_s[rows, :]
        cum_t = cum.T
        skip = par[2:3, :]
        scores = []
        for d in range(2):
            s = lax.dot_general(
                bc[rows, d * 256 + 128 : d * 256 + 256], bc[rows, d * 256 : d * 256 + 128],
                (((1,), (1,)), ((), ())), preferred_element_type=F32,
            )
            scores.append(jnp.where(lower if d == 0 else upper, s, 0.0))
        for g in range(8):
            values = jnp.concatenate([xdt[0, rows, lanes(g)], xdt[1, rows, lanes(g)]], axis=0)
            outs = []
            for k in range(2):
                w = []
                for d in range(2):
                    n = d * 16 + 2 * g + k
                    gap = jnp.minimum(cum[:, n : n + 1] - cum_t[n : n + 1, :], 0.0)
                    w.append((scores[d] * jnp.exp2(gap)).astype(BF))
                outs.append(dot(jnp.concatenate(w, axis=1), values))
            y = jnp.where(col_i < 64, outs[0], outs[1])
            for d in range(2):
                y = y + expand(skip, d * 16 + 2 * g) * xs[d, rows, lanes(g)].astype(F32)
            y_s[rows, lanes(g)] = y

    near.wait_recv()
    phase(hi, True)
    pass_on(0)
    for up, flag in ((True, first), (False, final)):

        @pl.when(jnp.logical_not(flag))
        def _(up=up):
            halo_copies(up)[0].wait_recv()

    forwarded(0).wait_recv()
    beside = pl.ds(pl.multiple_of(jnp.where(hi == 0, EDGE + HALF, HALF), 16), EDGE)
    edge[0:16, :] = tb[0:EDGE, :]
    edge[16:32, :] = tb[beside, :]
    edge[32:48, :] = tb[EDGE + TOK :, :]

    def put_edge(out, cols):
        out = out.astype(BF).astype(F32)
        xp[0:EDGE, cols] = out[0:16]
        xp[beside, cols] = out[16:32]
        xp[EDGE + TOK :, cols] = out[32:48]

    over(lambda: edge[...], wv, CH, 256, put_edge)

    @pl.loop(0, 2)
    def _(i):
        j = hi * 2 + i
        prepare(j)
        convolve(j)
        update(j)
        pass_on(1 + i)

    @pl.loop(0, 2)
    def _(i):
        intra(hi * 2 + i)

        @pl.when(i == 0)
        def _():
            pass_on(3)

    for i in range(1, CHUNKS):
        forwarded(i).wait_recv()
    phase(1 - hi, False)

    @pl.loop(0, 2)
    def _(i):
        j = (1 - hi) * 2 + i
        prepare(j)
        convolve(j)
        update(j)

    row8 = lax.broadcasted_iota(jnp.int32, (8, 128), 0)
    shrink = jnp.exp2(tot_s[...])
    whole = jnp.exp2(tot_s[0:1, :] + tot_s[1:2, :] + tot_s[2:3, :] + tot_s[3:4, :])
    for g in range(8):
        tail = jnp.zeros((8, 128), F32)
        for d in range(2):
            base = d * 16 + 2 * g
            decay = expand(whole, base)
            high = decay.astype(BF).astype(F32)
            tail = jnp.where(row8 == 2 * d, high, tail)
            tail = jnp.where(row8 == 2 * d + 1, decay - high, tail)
            order = range(NBLK) if d == 0 else range(NBLK - 1, -1, -1)
            state = None
            for j in order:
                new = upd[d, j, :, lanes(g)]
                if state is None:
                    state = new
                else:
                    start[d, j, :, lanes(g)] = state.astype(BF)
                    state = state * expand(shrink[j : j + 1], base) + new
            state = state.astype(BF)
            for r in range(4):
                msg[g * 4 + r, d * 32 : d * 32 + 32] = state[r * 32 : r * 32 + 32]
        for r in range(4):
            msg[g * 4 + r, 64:72] = tail.astype(BF)

    def everywhere(src, dst, send, recv):
        copies = []
        for i, peer in enumerate(peers):
            copy = remote(src.at[peer], dst.at[frame], send.at[i], recv.at[i], dev(peer, row))
            copy.start()
            copies.append(copy)
        dst[frame] = src[frame]
        return copies

    there = everywhere(msg, got, a_s, a_r)

    @pl.loop(0, 2)
    def _(i):
        intra((1 - hi) * 2 + i)

    for copy in there:
        copy.wait_recv()
    for d in range(2):
        state = jnp.zeros((32, 128), F32)
        for g in range(FRAMES) if d == 0 else reversed(range(FRAMES)):
            ret[g, d * 32 : d * 32 + 32] = state.astype(BF)
            tail = got[g, 64:72].astype(F32)
            decay = tail[2 * d : 2 * d + 1] + tail[2 * d + 1 : 2 * d + 2]
            state = decay * state + got[g, d * 32 : d * 32 + 32].astype(F32)
    back = everywhere(ret, inc, b_s, b_r)

    loads[5].wait()

    def put_gate(out, cols):
        gate[:, cols] = out.astype(BF)

    over(lambda: tb[EDGE : EDGE + TOK, :], wg, CH, 256, put_gate)

    def from_start(j, d):
        rows = block(j)
        grown = jnp.exp2(cum_s[rows, :])
        c = bc[rows, d * 256 + 128 : d * 256 + 256]
        for g in range(8):
            y_s[rows, lanes(g)] += expand(grown, d * 16 + 2 * g) * dot(c, start[d, j, :, lanes(g)])

    @pl.loop(0, NBLK - 1)
    def _(i):
        from_start(i + 1, 0)
        from_start(i, 1)

    zero = jnp.zeros((1, 128), F32)
    before, after = [zero], [zero]
    for j in range(NBLK - 1):
        before.append(before[-1] + tot_s[j : j + 1, :])
        after.append(after[-1] + tot_s[NBLK - 1 - j : NBLK - j, :])
    after = after[::-1]
    for j in range(NBLK):
        rows = slice(j * BLK, (j + 1) * BLK)
        ef_s[rows, :] = jnp.exp2(cum_s[rows, :] + jnp.where(fwd_lane[0:1], before[j], after[j]))
    for copy in back:
        copy.wait_recv()
    for g in range(8):
        for r in range(4):
            for d in range(2):
                inc_m[d, r * 32 : r * 32 + 32, lanes(g)] = inc[g * 4 + r, d * 32 : d * 32 + 32]

    def gated_rows(n, target):
        rows = block(target)
        ef = ef_s[rows, :]
        total = jnp.zeros((BLK, 1), F32)
        for g in range(8):
            y = y_s[rows, lanes(g)]
            for d in range(2):
                c = bc[rows, d * 256 + 128 : d * 256 + 256]
                y = y + expand(ef, d * 16 + 2 * g) * dot(c, inc_m[d, :, lanes(g)])
            gated = y * silu(gate[rows, lanes(g)].astype(F32))
            total = total + jnp.sum(gated * gated, axis=1, keepdims=True)
            normed[block(n), lanes(g)] = (gated * gain_ref[:, lanes(g)]).astype(BF)
        sq[n] = jnp.broadcast_to(total, (BLK, BLK)).T[0:8]

    @pl.loop(0, 2)
    def _(n):
        gated_rows(n, jnp.where(n == 0, corner, across))

    loads[6].wait()
    ones, twos, threes = [], [], []
    for k in range(NCOL):
        cols = slice(k * COLS, (k + 1) * COLS)
        part = dot(normed[0:HALF, :], wo[:, cols])
        to_partner[0, k] = part[0:BLK].astype(BF)
        copy = remote(
            to_partner.at[0, k], from_partner.at[0, k], f_s.at[k], f_r.at[k], dev(frame, partner)
        )
        copy.start()
        ones.append(copy)
        own[k] = part[BLK:]
    for k in range(NCOL):
        ones[k].wait_recv()
        to_across[k] = (own[k] + from_partner[0, k].astype(F32)).astype(BF)
        copy = remote(
            to_across.at[k], from_across.at[k], f_s.at[NCOL + k], f_r.at[NCOL + k],
            dev(frame, across),
        )
        copy.start()
        twos.append(copy)

    @pl.loop(2, 4)
    def _(n):
        gated_rows(n, jnp.where(n == 2, partner, row))

    sq_out[0] = sq[0]
    sq_out[1] = sq[2]
    sq_copy = remote(sq_out, sq_part, f_s.at[3 * NCOL], f_r.at[3 * NCOL], dev(frame, partner))
    sq_copy.start()
    for k in range(NCOL):
        cols = slice(k * COLS, (k + 1) * COLS)
        part = dot(normed[HALF:, :], wo[:, cols])
        to_partner[1, k] = part[0:BLK].astype(BF)
        copy = remote(
            to_partner.at[1, k], from_partner.at[1, k], f_s.at[2 * NCOL + k],
            f_r.at[2 * NCOL + k], dev(frame, partner),
        )
        copy.start()
        threes.append(copy)
        own[k] = part[BLK:]
    sq_copy.wait_recv()
    sq_cross[...] = sq[1] + sq_part[0]
    far_copy = remote(
        sq_cross, sq_far, f_s.at[3 * NCOL + 1], f_r.at[3 * NCOL + 1], dev(frame, across)
    )
    far_copy.start()
    for k in range(NCOL):
        threes[k].wait_recv()
        own[k] = own[k] + from_partner[1, k].astype(F32)
    far_copy.wait_recv()
    mean = (sq[3] + sq_part[1] + sq_far[...]) * (1.0 / D_INNER)
    scale = jnp.broadcast_to(lax.rsqrt(mean + 1e-05)[0:1], (BLK, BLK)).T[:, 0:1]
    for k in range(NCOL):
        cols = slice(k * COLS, (k + 1) * COLS)
        twos[k].wait_recv()
        out_ref[:, cols] = (scale * (own[k] + from_across[k].astype(F32))).astype(BF)

    near.wait_send()
    for i in range(CHUNKS):
        cross(i, row, hi).wait_send()
        forward(i).wait_send()
    for up, flag in ((True, to_next), (False, to_prev)):

        @pl.when(flag)
        def _(up=up):
            for copy in halo_copies(up):
                copy.wait_send()

    for copy in there + back + ones + twos + threes + [sq_copy, far_copy]:
        copy.wait_send()


def layer(*operands):
    dma = pltpu.SemaphoreType.DMA
    vmem = pltpu.VMEM
    return pl.pallas_call(
        layer_body,
        name="layer",
        out_shape=jax.ShapeDtypeStruct((BLK, D), BF),
        in_specs=[ANY] * 6 + [VM] * 5,
        out_specs=VM,
        scratch_shapes=[
            vmem((TOK + 2 * EDGE, D), BF), vmem((48, D), BF),
            vmem((D, CH), BF), vmem((D, CH), BF), vmem((D, 512), BF), vmem((128, D), BF),
            vmem((CH, D), BF), vmem((8, 128), F32), vmem((TOK, CH), BF), vmem((TOK, 512), BF),
            vmem((TOK + 2 * EDGE, CH), F32),
            vmem((2, TOK, CH), BF), vmem((2, TOK, CH), BF),
            vmem((2, NBLK, 128, CH), BF), vmem((2, NBLK, 128, CH), F32), vmem((BLK, CH), BF),
            vmem((TOK, 128), F32), vmem((TOK, 128), F32), vmem((8, 128), F32),
            vmem((TOK, CH), F32), vmem((TOK, 128), F32),
            vmem((FRAMES, MSG, 128), BF), vmem((FRAMES, MSG, 128), BF),
            vmem((FRAMES, 64, 128), BF), vmem((FRAMES, 64, 128), BF), vmem((2, 128, CH), BF),
            vmem((TOK, CH), BF), vmem((4, 8, 128), F32),
            vmem((2, NCOL, BLK, COLS), BF), vmem((2, NCOL, BLK, COLS), BF),
            vmem((NCOL, BLK, COLS), BF), vmem((NCOL, BLK, COLS), BF),
            vmem((NCOL, BLK, COLS), F32),
            vmem((2, 8, 128), F32), vmem((2, 8, 128), F32), vmem((8, 128), F32),
            vmem((8, 128), F32),
            dma((7,)), dma((2 * CHUNKS + 9,)), dma((2 * CHUNKS + 3,)),
            dma((PEERS,)), dma((PEERS,)), dma((PEERS,)), dma((PEERS,)),
            dma((3 * NCOL + 2,)), dma((3 * NCOL + 2,)),
        ],
        compiler_params=pltpu.CompilerParams(
            collective_id=0, has_side_effects=True, vmem_limit_bytes=62 * 1024 * 1024
        ),
    )(*operands)


def per_device(
    tokens, w_gate, w_value, w_state_proj, w_step, step_bias, decay_rate, conv_taps,
    skip_gain, norm_gain, w_out,
):
    out = layer(
        tokens[0], w_gate, w_value, w_state_proj, jnp.swapaxes(w_step, 1, 2), w_out,
        step_bias, decay_rate, skip_gain, conv_taps, norm_gain[None, :],
    )
    return out[None]


def solution(mesh):
    in_specs = (
        P("frame", "row", None), P(None, "row"), P(None, "row"), P(), P(None, None, "row"),
        P(None, "row"), P(None, "row"), P(None, None, "row"), P(None, "row"), P("row"),
        P("row", None),
    )
    return jax.shard_map(
        per_device, mesh=mesh, in_specs=in_specs, out_specs=P("frame", "row", None),
        check_vma=False,
    )
```

time: 327 us -> 76.5 us (0.23)
  blocking collectives: 87.7 us -> 0 us
  waiting for transfers between devices: 76.9 us -> 0 us
  Pallas kernels: 0 us -> 74.4 us
  matrix products: 57.6 us -> 0 us
  other arithmetic: 37 us -> 0 us
  local copies, waits for them, and re-layouts: 37.8 us -> 1.88 us
  between operations: 14.7 us -> 0.01 us
  starting transfers between devices: 12.9 us -> 0 us
    pallas_call x0 -> x1, Pallas kernels: none -> 74.4 us  [layer(): pl.pallas_call(layer_body, name='layer', out_shape=jax.ShapeDtypeStruct((...]
    dot_general x32 -> x0, matrix products: 57.6 us -> none  [the longest x8 18.5 us: advance(): jnp.einsum('hts,shp->thp', weights, x_block, preferred_element_type=jnp.f...]
    all_gather x4 -> x0, waiting for transfers between devices: 46.6 us -> none  [entering_2(): lax.all_gather(part.astype(kind), axis)]
    all_to_all x2 -> x0, blocking collectives: 41.8 us -> none  [the longest x1 30.2 us: summed_on_arrival(): lax.all_to_all(split_up(shard, dim, devices), axis, 0, 0, tiled=True)]
    all_gather x6 -> x0, blocking collectives: 41.4 us -> none  [entering_2(): lax.all_gather(part.astype(kind), axis)]
    all_to_all x1 -> x0, waiting for transfers between devices: 24.4 us -> none  [sent_to_all(): lax.all_to_all(jnp.broadcast_to(shard[None], (devices, *shard.shape)), ax...]
    convert_element_type x10 -> x0, other arithmetic: 14.5 us -> none  [the longest x8 7.07 us: entering_2(): part.astype(kind)]
    another operation x9 -> x0, local copies, waits for them, and re-layouts: 8.47 us -> none
  transfers between devices with their start and end apart: 7 -> 0, of which waited for: 6 -> 0; matrix products, arithmetic and copies ran while one was open for 8% -> 0% of each run, Pallas kernels for 0% -> 0%
where the time goes in v2:
time: 76.5 us; the launch traced here: 76.3 us
  Pallas kernels  74.4 us (97%)
  local copies, waits for them, and re-layouts  1.88 us (2%)
    pallas_call x1, Pallas kernels, layer(): pl.pallas_call(layer_body, name='layer', out_shape=jax.ShapeDtypeStruct((...  74.4 us
    unnamed x1, local copies, waits for them, and re-layouts  1.88 us

profile of v2, /device:TPU:1, one launch (start us, length us, event | category | flops | bytes accessed | tf_op | source)
XLA Modules:
  0.0 76.3 jit_solution(12094837739937983038)
XLA Ops:
  0.0 74.4 %layer.1 = bf16[128,2048]{1,0:T(8,128)(2,1)} custom-call(bf16[128,2048]{1,0:T(8,128)(2,1)} %bitcast.5, bf16[2048,1024]{1,0:T(8,128)(2,1)} %wg_ref.1, bf16[2048,1024]{1,0:T(8,128)(2,1)} %wv_ref.1, bf16[2048,512]{1,0:T(8,128)(2,1)} %ws_ref.1, bf16[2,16,2048]{2,1,0:T(8,128)(2,1)} %bitcast.6, bf16[1024,2048]{1,0:T(8,128)(2,1)} %wo_ref.1, f32[2,16]{1,0:T(2,128)} %bias_ref.1, ...), custom_call_target="tpu_custom_call" | custom-call | tf_op jit(solution)/shard_map/layer/pallas_call | solution.py:515
  74.4 1.9 %copy.13 = bf16[1,128,2048]{2,1,0:T(8,128)(2,1)} copy(bf16[1,128,2048]{2,1,0:T(8,128)(2,1)} %bitcast.4) | data formatting | bytes 1048576

commit v3 on v2

--- a/solution.py
+++ b/solution.py
@@ -48,8 +48,13 @@
 CROWS = 128 // CHUNKS
 EDGE = 16
 COLS = 512
+LAG = 2
 NCOL = D // COLS
 PEERS = FRAMES - 1
+STEPS = sorted(
+    ((dx, dy, dz) for dx in range(4) for dy in range(4) for dz in range(2) if dx + dy + dz),
+    key=lambda s: -(min(s[0], 4 - s[0]) + min(s[1], 4 - s[1]) + s[2]),
+)
 
 
 def expand(values, base):
@@ -70,7 +75,7 @@
     bias_ref, rate_ref, skip_ref, taps_ref, gain_ref,
     out_ref,
     tb, edge, wg, wv, ws, wt, wo, par, gate, bc,
-    xp, xs, xdt, start, upd, car, cum_s, dt_s, tot_s, y_s, ef_s,
+    xp, xs, start, upd, car, cum_s, dt_s, tot_s, y_s, ef_s, off_s,
     msg, got, ret, inc, inc_m,
     normed, sq, to_partner, from_partner, to_across, from_across, own,
     sq_out, sq_part, sq_cross, sq_far,
@@ -80,7 +85,11 @@
     partner = row + 1 - 2 * core
     across = lax.rem(row + 2, 4)
     corner = lax.rem(partner + 2, 4)
-    peers = [lax.rem(frame + i, FRAMES) for i in range(1, FRAMES)]
+    fx, fy, fz = lax.div(frame, 8), lax.rem(lax.div(frame, 2), 4), lax.rem(frame, 2)
+    peers = [
+        lax.rem(fx + dx, 4) * 8 + lax.rem(fy + dy, 4) * 2 + lax.rem(fz + dz, 2)
+        for dx, dy, dz in STEPS
+    ]
     first, final = frame == 0, frame == FRAMES - 1
 
     mine = pl.ds(pl.multiple_of(EDGE + row * BLK, 16), BLK)
@@ -186,18 +195,25 @@
         rows = pl.ds(pl.multiple_of(half * HALF, 16), HALF)
         rows_x = pl.ds(pl.multiple_of(EDGE + half * HALF, 16), HALF)
 
+        def read_x():
+            return read() if waits else jnp.concatenate([read(), edge[...]], axis=0)
+
         def put_x(out, cols):
-            xp[rows_x, cols] = out.astype(BF).astype(F32)
+            out = out.astype(BF).astype(F32)
+            xp[rows_x, cols] = out[:HALF]
+            if not waits:
+                xp[0:EDGE, cols] = out[HALF : HALF + EDGE]
+                xp[EDGE + TOK :, cols] = out[HALF + EDGE :]
 
         def put_bc(out, cols):
             bc[rows, cols] = out.astype(BF)
 
         if waits:
             loads[1].wait()
-        over(read, wv, CH, 256, put_x)
+        over(read_x, wv, CH, 512, put_x)
         if waits:
             loads[2].wait()
-        over(read, ws, 512, 256, put_bc)
+        over(read, ws, 512, 512, put_bc)
         if waits:
             loads[3].wait()
             loads[4].wait()
@@ -224,40 +240,28 @@
         cum_s[rows, :] = jnp.where(fwd_lane, cum, (total - cum) + part)
         tot_s[pl.ds(j, 1), :] = total
 
-    def convolve(j):
+    def scan_in(j, d):
+        size = BLK + 2 * EDGE
+        rows = block(j)
+        fade = jnp.exp2(tot_s[pl.ds(j, 1), :] - cum_s[rows, :]) * dt_s[rows, :]
+        bt = bc[rows, d * 256 : d * 256 + 128].astype(F32).T.astype(BF)
         for g in range(8):
-            window = xp[block(j, BLK + 2 * EDGE), lanes(g)]
-            size = BLK + 2 * EDGE
-            shifted = {
-                o: pltpu.roll(window, (-o) % size, 0)[EDGE : EDGE + BLK] if o
-                else window[EDGE : EDGE + BLK]
-                for o in range(-3, 4)
-            }
-            for d in range(2):
-                acc = None
-                for k in range(4):
-                    term = taps_ref[d, k : k + 1, lanes(g)] * shifted[3 - k if d else k - 3]
-                    acc = term if acc is None else acc + term
-                xs[d, block(j), lanes(g)] = silu(acc).astype(BF)
-
-    def update(j):
-        rows = block(j)
-        total = tot_s[pl.ds(j, 1), :]
-        dt_j = dt_s[rows, :]
-        fade = jnp.exp2(total - cum_s[rows, :]) * dt_j
-        for d in range(2):
-            b = bc[rows, d * 256 : d * 256 + 128]
-            bt = b.astype(F32).T.astype(BF)
-            for g in range(8):
-                x = xs[d, rows, lanes(g)].astype(F32)
-                xdt[d, rows, lanes(g)] = (x * expand(dt_j, d * 16 + 2 * g)).astype(BF)
-                carried = (x * expand(fade, d * 16 + 2 * g)).astype(BF)
-                upd[d, pl.ds(j, 1), :, lanes(g)] = dot(bt, carried)[None]
+            window = xp[block(j, size), lanes(g)]
+            acc = None
+            for k in range(4):
+                o = 3 - k if d else k - 3
+                moved = pltpu.roll(window, (-o) % size, 0) if o else window
+                term = taps_ref[d, k : k + 1, lanes(g)] * moved[EDGE : EDGE + BLK]
+                acc = term if acc is None else acc + term
+            x = silu(acc).astype(BF)
+            xs[d, rows, lanes(g)] = x
+            carried = (x.astype(F32) * expand(fade, d * 16 + 2 * g)).astype(BF)
+            upd[d, pl.ds(j, 1), :, lanes(g)] = dot(bt, carried)[None]
 
     def intra(j):
         rows = block(j)
         cum = cum_s[rows, :]
-        cum_t = cum.T
+        cum_t, dt_t = cum.T, dt_s[rows, :].T
         skip = par[2:3, :]
         scores = []
         for d in range(2):
@@ -267,14 +271,14 @@
             )
             scores.append(jnp.where(lower if d == 0 else upper, s, 0.0))
         for g in range(8):
-            values = jnp.concatenate([xdt[0, rows, lanes(g)], xdt[1, rows, lanes(g)]], axis=0)
+            values = jnp.concatenate([xs[0, rows, lanes(g)], xs[1, rows, lanes(g)]], axis=0)
             outs = []
             for k in range(2):
                 w = []
                 for d in range(2):
                     n = d * 16 + 2 * g + k
                     gap = jnp.minimum(cum[:, n : n + 1] - cum_t[n : n + 1, :], 0.0)
-                    w.append((scores[d] * jnp.exp2(gap)).astype(BF))
+                    w.append((scores[d] * jnp.exp2(gap) * dt_t[n : n + 1, :]).astype(BF))
                 outs.append(dot(jnp.concatenate(w, axis=1), values))
             y = jnp.where(col_i < 64, outs[0], outs[1])
             for d in range(2):
@@ -284,52 +288,50 @@
     near.wait_recv()
     phase(hi, True)
     pass_on(0)
+    forwarded(0).wait_recv()
+    beside = pl.ds(pl.multiple_of(jnp.where(hi == 0, EDGE + HALF, HALF), 16), EDGE)
+
+    def put_edge(out, cols):
+        xp[beside, cols] = out.astype(BF).astype(F32)
+
+    over(lambda: tb[beside, :], wv, CH, 512, put_edge)
+
+    prepare(hi * 2)
+    prepare(hi * 2 + 1)
+    for d in range(2):
+        scan_in(1 + hi, d)
+        pass_on(1 + d)
+    for h in range(2):
+
+        @pl.when(hi == h)
+        def _(h=h):
+            scan_in(3 * h, 1 - h)
+
+    pass_on(3)
+    for i in range(1, CHUNKS):
+        forwarded(i).wait_recv()
     for up, flag in ((True, first), (False, final)):
 
         @pl.when(jnp.logical_not(flag))
         def _(up=up):
             halo_copies(up)[0].wait_recv()
 
-    forwarded(0).wait_recv()
-    beside = pl.ds(pl.multiple_of(jnp.where(hi == 0, EDGE + HALF, HALF), 16), EDGE)
     edge[0:16, :] = tb[0:EDGE, :]
-    edge[16:32, :] = tb[beside, :]
-    edge[32:48, :] = tb[EDGE + TOK :, :]
-
-    def put_edge(out, cols):
-        out = out.astype(BF).astype(F32)
-        xp[0:EDGE, cols] = out[0:16]
-        xp[beside, cols] = out[16:32]
-        xp[EDGE + TOK :, cols] = out[32:48]
-
-    over(lambda: edge[...], wv, CH, 256, put_edge)
-
-    @pl.loop(0, 2)
-    def _(i):
-        j = hi * 2 + i
-        prepare(j)
-        convolve(j)
-        update(j)
-        pass_on(1 + i)
-
-    @pl.loop(0, 2)
-    def _(i):
-        intra(hi * 2 + i)
-
-        @pl.when(i == 0)
-        def _():
-            pass_on(3)
-
-    for i in range(1, CHUNKS):
-        forwarded(i).wait_recv()
+    edge[16:32, :] = tb[EDGE + TOK :, :]
     phase(1 - hi, False)
 
     @pl.loop(0, 2)
     def _(i):
         j = (1 - hi) * 2 + i
         prepare(j)
-        convolve(j)
-        update(j)
+        for d in range(2):
+            scan_in(j, d)
+
+    for h in range(2):
+
+        @pl.when(hi == h)
+        def _(h=h):
+            scan_in(3 * h, h)
 
     row8 = lax.broadcasted_iota(jnp.int32, (8, 128), 0)
     shrink = jnp.exp2(tot_s[...])
@@ -368,9 +370,9 @@
 
     there = everywhere(msg, got, a_s, a_r)
 
-    @pl.loop(0, 2)
+    @pl.loop(0, NBLK)
     def _(i):
-        intra((1 - hi) * 2 + i)
+        intra(i)
 
     for copy in there:
         copy.wait_recv()
@@ -388,7 +390,7 @@
     def put_gate(out, cols):
         gate[:, cols] = out.astype(BF)
 
-    over(lambda: tb[EDGE : EDGE + TOK, :], wg, CH, 256, put_gate)
+    over(lambda: tb[EDGE : EDGE + TOK, :], wg, CH, 512, put_gate)
 
     def from_start(j, d):
         rows = block(j)
@@ -409,8 +411,21 @@
         after.append(after[-1] + tot_s[NBLK - 1 - j : NBLK - j, :])
     after = after[::-1]
     for j in range(NBLK):
-        rows = slice(j * BLK, (j + 1) * BLK)
-        ef_s[rows, :] = jnp.exp2(cum_s[rows, :] + jnp.where(fwd_lane[0:1], before[j], after[j]))
+        off_s[j : j + 1, :] = jnp.where(fwd_lane[0:1], before[j], after[j])
+
+    @pl.loop(0, NBLK)
+    def _(n):
+        target = jnp.where(
+            n == 0, corner, jnp.where(n == 1, across, jnp.where(n == 2, partner, row))
+        )
+        rows = block(target)
+        ef = jnp.exp2(cum_s[rows, :] + off_s[pl.ds(target, 1), :])
+        for g in range(8):
+            open_g = silu(gate[rows, lanes(g)].astype(F32))
+            y_s[rows, lanes(g)] = y_s[rows, lanes(g)] * open_g
+            for d in range(2):
+                ef_s[d, block(n), lanes(g)] = open_g * expand(ef, d * 16 + 2 * g)
+
     for copy in back:
         copy.wait_recv()
     for g in range(8):
@@ -420,17 +435,15 @@
 
     def gated_rows(n, target):
         rows = block(target)
-        ef = ef_s[rows, :]
-        total = jnp.zeros((BLK, 1), F32)
+        total = jnp.zeros((BLK, BLK), F32)
         for g in range(8):
-            y = y_s[rows, lanes(g)]
+            gated = y_s[rows, lanes(g)]
             for d in range(2):
                 c = bc[rows, d * 256 + 128 : d * 256 + 256]
-                y = y + expand(ef, d * 16 + 2 * g) * dot(c, inc_m[d, :, lanes(g)])
-            gated = y * silu(gate[rows, lanes(g)].astype(F32))
-            total = total + jnp.sum(gated * gated, axis=1, keepdims=True)
+                gated = gated + ef_s[d, block(n), lanes(g)] * dot(c, inc_m[d, :, lanes(g)])
+            total = total + gated * gated
             normed[block(n), lanes(g)] = (gated * gain_ref[:, lanes(g)]).astype(BF)
-        sq[n] = jnp.broadcast_to(total, (BLK, BLK)).T[0:8]
+        sq[n] = jnp.broadcast_to(jnp.sum(total.T, axis=0, keepdims=True), (8, BLK))
 
     @pl.loop(0, 2)
     def _(n):
@@ -438,6 +451,17 @@
 
     loads[6].wait()
     ones, twos, threes = [], [], []
+
+    def relay(k):
+        ones[k].wait_recv()
+        to_across[k] = (own[k] + from_partner[0, k].astype(F32)).astype(BF)
+        copy = remote(
+            to_across.at[k], from_across.at[k], f_s.at[NCOL + k], f_r.at[NCOL + k],
+            dev(frame, across),
+        )
+        copy.start()
+        twos.append(copy)
+
     for k in range(NCOL):
         cols = slice(k * COLS, (k + 1) * COLS)
         part = dot(normed[0:HALF, :], wo[:, cols])
@@ -448,16 +472,10 @@
         copy.start()
         ones.append(copy)
         own[k] = part[BLK:]
-    for k in range(NCOL):
-        ones[k].wait_recv()
-        to_across[k] = (own[k] + from_partner[0, k].astype(F32)).astype(BF)
-        copy = remote(
-            to_across.at[k], from_across.at[k], f_s.at[NCOL + k], f_r.at[NCOL + k],
-            dev(frame, across),
-        )
-        copy.start()
-        twos.append(copy)
-
+        if k >= LAG:
+            relay(k - LAG)
+    for k in range(NCOL - LAG, NCOL):
+        relay(k)
     @pl.loop(2, 4)
     def _(n):
         gated_rows(n, jnp.where(n == 2, partner, row))
@@ -519,14 +537,14 @@
         in_specs=[ANY] * 6 + [VM] * 5,
         out_specs=VM,
         scratch_shapes=[
-            vmem((TOK + 2 * EDGE, D), BF), vmem((48, D), BF),
+            vmem((TOK + 2 * EDGE, D), BF), vmem((32, D), BF),
             vmem((D, CH), BF), vmem((D, CH), BF), vmem((D, 512), BF), vmem((128, D), BF),
             vmem((CH, D), BF), vmem((8, 128), F32), vmem((TOK, CH), BF), vmem((TOK, 512), BF),
             vmem((TOK + 2 * EDGE, CH), F32),
-            vmem((2, TOK, CH), BF), vmem((2, TOK, CH), BF),
+            vmem((2, TOK, CH), BF),
             vmem((2, NBLK, 128, CH), BF), vmem((2, NBLK, 128, CH), F32), vmem((BLK, CH), BF),
             vmem((TOK, 128), F32), vmem((TOK, 128), F32), vmem((8, 128), F32),
-            vmem((TOK, CH), F32), vmem((TOK, 128), F32),
+            vmem((TOK, CH), F32), vmem((2, TOK, CH), F32), vmem((8, 128), F32),
             vmem((FRAMES, MSG, 128), BF), vmem((FRAMES, MSG, 128), BF),
             vmem((FRAMES, 64, 128), BF), vmem((FRAMES, 64, 128), BF), vmem((2, 128, CH), BF),
             vmem((TOK, CH), BF), vmem((4, 8, 128), F32),

time: 76.5 us -> 69.6 us (0.910)
  Pallas kernels: 74.4 us -> 67.5 us
    pallas_call x1, Pallas kernels: 74.4 us -> 67.5 us  [layer(): pl.pallas_call(layer_body, name='layer', out_shape=jax.ShapeDtypeStruct((...]
where the time goes in v3:
time: 69.6 us; the launch traced here: 69.4 us
  Pallas kernels  67.5 us (97%)
  local copies, waits for them, and re-layouts  1.88 us (3%)
    pallas_call x1, Pallas kernels, layer(): pl.pallas_call(layer_body, name='layer', out_shape=jax.ShapeDtypeStruct((...  67.5 us
    unnamed x1, local copies, waits for them, and re-layouts  1.88 us

profile of v3, /device:TPU:1, one launch (start us, length us, event | category | flops | bytes accessed | tf_op | source)
XLA Modules:
  0.0 69.4 jit_solution(18031637697066843140)
XLA Ops:
  0.0 67.5 %layer.1 = bf16[128,2048]{1,0:T(8,128)(2,1)} custom-call(bf16[128,2048]{1,0:T(8,128)(2,1)} %bitcast.5, bf16[2048,1024]{1,0:T(8,128)(2,1)} %wg_ref.1, bf16[2048,1024]{1,0:T(8,128)(2,1)} %wv_ref.1, bf16[2048,512]{1,0:T(8,128)(2,1)} %ws_ref.1, bf16[2,16,2048]{2,1,0:T(8,128)(2,1)} %bitcast.6, bf16[1024,2048]{1,0:T(8,128)(2,1)} %wo_ref.1, f32[2,16]{1,0:T(2,128)} %bias_ref.1, ...), custom_call_target="tpu_custom_call" | custom-call | tf_op jit(solution)/shard_map/layer/pallas_call | solution.py:533
  67.5 1.9 %copy.13 = bf16[1,128,2048]{2,1,0:T(8,128)(2,1)} copy(bf16[1,128,2048]{2,1,0:T(8,128)(2,1)} %bitcast.4) | data formatting | bytes 1048576

commit v4 on v3

--- a/solution.py
+++ b/solution.py
@@ -46,6 +46,7 @@
 
 CHUNKS = 4
 CROWS = 128 // CHUNKS
+HALF_BLK = 64
 EDGE = 16
 COLS = 512
 LAG = 2
@@ -130,28 +131,29 @@
         barrier, 2 + PEERS + jnp.where(jnp.logical_or(to_next, to_prev), 4, 0)
     )
 
-    def chunk_rows(owner, i, sender_hi):
-        at = jnp.where(sender_hi == 1, i, CHUNKS - 1 - i) * CROWS
-        return pl.ds(pl.multiple_of(EDGE + owner * BLK + at, 16), CROWS)
-
-    def cross(i, owner, sender_hi):
-        rows = chunk_rows(owner, i, sender_hi)
+    def chunk_rows(sender, i, side):
+        at = jnp.where(side == 1, i % 2, 1 - i % 2) * CROWS + sender * HALF_BLK
+        source = 1 + side if i < 2 else 3 * side
+        return pl.ds(pl.multiple_of(EDGE + source * BLK + at, 16), CROWS)
+
+    def cross(i, side):
+        rows = chunk_rows(core, i, side)
         return remote(tb.at[rows], tb.at[rows], g_s.at[i], g_r.at[i], dev(frame, across))
 
-    def forward(i):
-        rows = chunk_rows(across, i, 1 - hi)
+    def over_chip(i, sender):
+        rows = chunk_rows(sender, i, 1 - hi)
         return remote(
             tb.at[rows], tb.at[rows], g_s.at[CHUNKS + i], g_r.at[CHUNKS + i], dev(frame, partner)
         )
 
+    def forward(i):
+        return over_chip(i, core)
+
     def forwarded(i):
-        rows = chunk_rows(corner, i, 1 - hi)
-        return remote(
-            tb.at[rows], tb.at[rows], g_s.at[CHUNKS + i], g_r.at[CHUNKS + i], dev(frame, partner)
-        )
+        return over_chip(i, 1 - core)
 
     def pass_on(i):
-        cross(i, across, 1 - hi).wait_recv()
+        cross(i, 1 - hi).wait_recv()
         forward(i).start()
 
     near = remote(
@@ -171,16 +173,18 @@
         ]
 
     near.start()
-    cross(0, row, hi).start()
+
+    @pl.when(core == 1 - hi)
+    def _():
+        cross(0, hi).start()
+        cross(1, hi).start()
+
     for up, flag in ((True, to_next), (False, to_prev)):
 
         @pl.when(flag)
         def _(up=up):
             for copy in halo_copies(up):
                 copy.start()
-
-    for i in range(1, CHUNKS):
-        cross(i, row, hi).start()
 
     def over(read, weight, columns, width, store):
         @pl.loop(0, columns // width)
@@ -188,22 +192,22 @@
             cols = pl.ds(pl.multiple_of(n * width, width), width)
             store(dot(read(), weight[:, cols]), cols)
 
-    def phase(half, waits):
+    def phase(base, count, waits, ends):
+        rows = pl.ds(pl.multiple_of(base, 16), count)
+        rows_x = pl.ds(pl.multiple_of(EDGE + base, 16), count)
+
         def read():
-            return tb[pl.ds(pl.multiple_of(EDGE + half * HALF, 16), HALF), :]
-
-        rows = pl.ds(pl.multiple_of(half * HALF, 16), HALF)
-        rows_x = pl.ds(pl.multiple_of(EDGE + half * HALF, 16), HALF)
+            return tb[rows_x, :]
 
         def read_x():
-            return read() if waits else jnp.concatenate([read(), edge[...]], axis=0)
+            return jnp.concatenate([read(), edge[...]], axis=0) if ends else read()
 
         def put_x(out, cols):
             out = out.astype(BF).astype(F32)
-            xp[rows_x, cols] = out[:HALF]
-            if not waits:
-                xp[0:EDGE, cols] = out[HALF : HALF + EDGE]
-                xp[EDGE + TOK :, cols] = out[HALF + EDGE :]
+            xp[rows_x, cols] = out[:count]
+            if ends:
+                xp[0:EDGE, cols] = out[count : count + EDGE]
+                xp[EDGE + TOK :, cols] = out[count + EDGE :]
 
         def put_bc(out, cols):
             bc[rows, cols] = out.astype(BF)
@@ -286,9 +290,23 @@
             y_s[rows, lanes(g)] = y
 
     near.wait_recv()
-    phase(hi, True)
-    pass_on(0)
-    forwarded(0).wait_recv()
+
+    @pl.when(core != 1 - hi)
+    def _():
+        cross(0, hi).start()
+        cross(1, hi).start()
+
+    cross(2, hi).start()
+    cross(3, hi).start()
+    phase(hi * HALF, HALF, True, False)
+    @pl.when(core == hi)
+    def _():
+        pass_on(0)
+
+    @pl.when(core != hi)
+    def _():
+        forwarded(0).wait_recv()
+
     beside = pl.ds(pl.multiple_of(jnp.where(hi == 0, EDGE + HALF, HALF), 16), EDGE)
 
     def put_edge(out, cols):
@@ -298,18 +316,37 @@
 
     prepare(hi * 2)
     prepare(hi * 2 + 1)
-    for d in range(2):
-        scan_in(1 + hi, d)
-        pass_on(1 + d)
+    scan_in(1 + hi, 0)
+
+    @pl.when(core != hi)
+    def _():
+        pass_on(0)
+
+    pass_on(1)
+    scan_in(1 + hi, 1)
     for h in range(2):
 
         @pl.when(hi == h)
         def _(h=h):
             scan_in(3 * h, 1 - h)
 
+    @pl.when(core == hi)
+    def _():
+        forwarded(0).wait_recv()
+
+    forwarded(1).wait_recv()
+    phase((2 - hi) * BLK, BLK, False, False)
+    prepare(2 - hi)
+    pass_on(2)
+    for h in range(2):
+
+        @pl.when(hi == h)
+        def _(h=h):
+            scan_in(2 - h, h)
+
     pass_on(3)
-    for i in range(1, CHUNKS):
-        forwarded(i).wait_recv()
+    forwarded(2).wait_recv()
+    forwarded(3).wait_recv()
     for up, flag in ((True, first), (False, final)):
 
         @pl.when(jnp.logical_not(flag))
@@ -318,19 +355,15 @@
 
     edge[0:16, :] = tb[0:EDGE, :]
     edge[16:32, :] = tb[EDGE + TOK :, :]
-    phase(1 - hi, False)
-
-    @pl.loop(0, 2)
-    def _(i):
-        j = (1 - hi) * 2 + i
-        prepare(j)
-        for d in range(2):
-            scan_in(j, d)
-
+    phase((1 - hi) * 3 * BLK, BLK, False, True)
+    prepare((1 - hi) * 3)
+    for d in range(2):
+        scan_in((1 - hi) * 3, d)
     for h in range(2):
 
         @pl.when(hi == h)
         def _(h=h):
+            scan_in(2 - h, 1 - h)
             scan_in(3 * h, h)
 
     row8 = lax.broadcasted_iota(jnp.int32, (8, 128), 0)
@@ -374,6 +407,13 @@
     def _(i):
         intra(i)
 
+    loads[5].wait()
+
+    def put_gate(out, cols):
+        gate[:, cols] = out.astype(BF)
+
+    over(lambda: tb[EDGE : EDGE + TOK, :], wg, CH, 512, put_gate)
+
     for copy in there:
         copy.wait_recv()
     for d in range(2):
@@ -384,13 +424,6 @@
             decay = tail[2 * d : 2 * d + 1] + tail[2 * d + 1 : 2 * d + 2]
             state = decay * state + got[g, d * 32 : d * 32 + 32].astype(F32)
     back = everywhere(ret, inc, b_s, b_r)
-
-    loads[5].wait()
-
-    def put_gate(out, cols):
-        gate[:, cols] = out.astype(BF)
-
-    over(lambda: tb[EDGE : EDGE + TOK, :], wg, CH, 512, put_gate)
 
     def from_start(j, d):
         rows = block(j)
@@ -514,7 +547,7 @@
 
     near.wait_send()
     for i in range(CHUNKS):
-        cross(i, row, hi).wait_send()
+        cross(i, hi).wait_send()
         forward(i).wait_send()
     for up, flag in ((True, to_next), (False, to_prev)):
 

time: 69.6 us -> 68.7 us (0.987)
  Pallas kernels: 67.5 us -> 66.6 us
    pallas_call x1, Pallas kernels: 67.5 us -> 66.6 us  [layer(): pl.pallas_call(layer_body, name='layer', out_shape=jax.ShapeDtypeStruct((...]
where the time goes in v4:
time: 68.7 us; the launch traced here: 68.5 us
  Pallas kernels  66.6 us (97%)
  local copies, waits for them, and re-layouts  1.88 us (3%)
    pallas_call x1, Pallas kernels, layer(): pl.pallas_call(layer_body, name='layer', out_shape=jax.ShapeDtypeStruct((...  66.6 us
    unnamed x1, local copies, waits for them, and re-layouts  1.88 us

profile of v4, /device:TPU:1, one launch (start us, length us, event | category | flops | bytes accessed | tf_op | source)
XLA Modules:
  0.0 68.5 jit_solution(17078263784812107034)
XLA Ops:
  0.0 66.6 %layer.1 = bf16[128,2048]{1,0:T(8,128)(2,1)} custom-call(bf16[128,2048]{1,0:T(8,128)(2,1)} %bitcast.5, bf16[2048,1024]{1,0:T(8,128)(2,1)} %wg_ref.1, bf16[2048,1024]{1,0:T(8,128)(2,1)} %wv_ref.1, bf16[2048,512]{1,0:T(8,128)(2,1)} %ws_ref.1, bf16[2,16,2048]{2,1,0:T(8,128)(2,1)} %bitcast.6, bf16[1024,2048]{1,0:T(8,128)(2,1)} %wo_ref.1, f32[2,16]{1,0:T(2,128)} %bias_ref.1, ...), custom_call_target="tpu_custom_call" | custom-call | tf_op jit(solution)/shard_map/layer/pallas_call | solution.py:566
  66.6 1.9 %copy.13 = bf16[1,128,2048]{2,1,0:T(8,128)(2,1)} copy(bf16[1,128,2048]{2,1,0:T(8,128)(2,1)} %bitcast.4) | data formatting | bytes 1048576

commit v5 on v4

--- a/solution.py
+++ b/solution.py
@@ -49,7 +49,7 @@
 HALF_BLK = 64
 EDGE = 16
 COLS = 512
-LAG = 2
+LAG = 1
 NCOL = D // COLS
 PEERS = FRAMES - 1
 STEPS = sorted(
@@ -73,8 +73,9 @@
 
 def layer_body(
     tok_ref, wg_ref, wv_ref, ws_ref, wt_ref, wo_ref,
+    bias_in, rate_in, skip_in, taps_in, gain_in,
+    out_ref,
     bias_ref, rate_ref, skip_ref, taps_ref, gain_ref,
-    out_ref,
     tb, edge, wg, wv, ws, wt, wo, par, gate, bc,
     xp, xs, start, upd, car, cum_s, dt_s, tot_s, y_s, ef_s, off_s,
     msg, got, ret, inc, inc_m,
@@ -96,9 +97,9 @@
     mine = pl.ds(pl.multiple_of(EDGE + row * BLK, 16), BLK)
     loads = []
     for i, (src, dst) in enumerate((
-        (tok_ref, tb.at[mine]), (wv_ref, wv), (ws_ref, ws),
-        (wt_ref.at[0], wt.at[0:16]), (wt_ref.at[1], wt.at[16:32]),
-        (wg_ref, wg), (wo_ref, wo),
+        (tok_ref, tb.at[mine]), (bias_in, bias_ref), (rate_in, rate_ref), (skip_in, skip_ref),
+        (wv_ref, wv), (ws_ref, ws), (wt_ref.at[0], wt.at[0:16]), (wt_ref.at[1], wt.at[16:32]),
+        (taps_in, taps_ref), (gain_in, gain_ref), (wg_ref, wg), (wo_ref, wo),
     )):
         copy = pltpu.make_async_copy(src, dst, w_sem.at[i])
         copy.start()
@@ -123,9 +124,6 @@
     to_prev = jnp.logical_and(row == 0, jnp.logical_not(first))
     wt[32:128, :] = jnp.zeros((96, D), BF)
     par[...] = jnp.zeros_like(par)
-    for i, ref in enumerate((bias_ref, rate_ref, skip_ref)):
-        for d in range(2):
-            par[i : i + 1, d * 16 : d * 16 + 16] = ref[d : d + 1, :]
     loads[0].wait()
     pl.semaphore_wait(
         barrier, 2 + PEERS + jnp.where(jnp.logical_or(to_next, to_prev), 4, 0)
@@ -213,14 +211,16 @@
             bc[rows, cols] = out.astype(BF)
 
         if waits:
-            loads[1].wait()
+            loads[4].wait()
         over(read_x, wv, CH, 512, put_x)
         if waits:
-            loads[2].wait()
+            loads[5].wait()
         over(read, ws, 512, 512, put_bc)
         if waits:
-            loads[3].wait()
-            loads[4].wait()
+            loads[6].wait()
+            loads[7].wait()
+            loads[8].wait()
+            loads[9].wait()
         raw = lax.dot_general(
             read(), wt[...], (((1,), (1,)), ((), ())), preferred_element_type=F32
         ).astype(BF).astype(F32) + par[0:1, :]
@@ -289,6 +289,11 @@
                 y = y + expand(skip, d * 16 + 2 * g) * xs[d, rows, lanes(g)].astype(F32)
             y_s[rows, lanes(g)] = y
 
+    for i in range(1, 4):
+        loads[i].wait()
+    for i, ref in enumerate((bias_ref, rate_ref, skip_ref)):
+        for d in range(2):
+            par[i : i + 1, d * 16 : d * 16 + 16] = ref[d : d + 1, :]
     near.wait_recv()
 
     @pl.when(core != 1 - hi)
@@ -407,7 +412,7 @@
     def _(i):
         intra(i)
 
-    loads[5].wait()
+    loads[10].wait()
 
     def put_gate(out, cols):
         gate[:, cols] = out.astype(BF)
@@ -482,7 +487,7 @@
     def _(n):
         gated_rows(n, jnp.where(n == 0, corner, across))
 
-    loads[6].wait()
+    loads[11].wait()
     ones, twos, threes = [], [], []
 
     def relay(k):
@@ -567,9 +572,11 @@
         layer_body,
         name="layer",
         out_shape=jax.ShapeDtypeStruct((BLK, D), BF),
-        in_specs=[ANY] * 6 + [VM] * 5,
+        in_specs=[ANY] * 11,
         out_specs=VM,
         scratch_shapes=[
+            vmem((2, 16), F32), vmem((2, 16), F32), vmem((2, 16), F32), vmem((2, 4, CH), F32),
+            vmem((1, CH), F32),
             vmem((TOK + 2 * EDGE, D), BF), vmem((32, D), BF),
             vmem((D, CH), BF), vmem((D, CH), BF), vmem((D, 512), BF), vmem((128, D), BF),
             vmem((CH, D), BF), vmem((8, 128), F32), vmem((TOK, CH), BF), vmem((TOK, 512), BF),
@@ -586,7 +593,7 @@
             vmem((NCOL, BLK, COLS), F32),
             vmem((2, 8, 128), F32), vmem((2, 8, 128), F32), vmem((8, 128), F32),
             vmem((8, 128), F32),
-            dma((7,)), dma((2 * CHUNKS + 9,)), dma((2 * CHUNKS + 3,)),
+            dma((12,)), dma((2 * CHUNKS + 9,)), dma((2 * CHUNKS + 3,)),
             dma((PEERS,)), dma((PEERS,)), dma((PEERS,)), dma((PEERS,)),
             dma((3 * NCOL + 2,)), dma((3 * NCOL + 2,)),
         ],

time: 68.7 us -> 67.7 us (0.985)
  Pallas kernels: 66.6 us -> 65.7 us
    pallas_call x1, Pallas kernels: 66.6 us -> 65.7 us  [layer(): pl.pallas_call(layer_body, name='layer', out_shape=jax.ShapeDtypeStruct((...]
where the time goes in v5:
time: 67.7 us; the launch traced here: 67.6 us
  Pallas kernels  65.7 us (97%)
  local copies, waits for them, and re-layouts  1.88 us (3%)
    pallas_call x1, Pallas kernels, layer(): pl.pallas_call(layer_body, name='layer', out_shape=jax.ShapeDtypeStruct((...  65.7 us
    unnamed x1, local copies, waits for them, and re-layouts  1.88 us

profile of v5, /device:TPU:1, one launch (start us, length us, event | category | flops | bytes accessed | tf_op | source)
XLA Modules:
  0.0 67.6 jit_solution(13113404733635261570)
XLA Ops:
  0.0 65.7 %layer.1 = bf16[128,2048]{1,0:T(8,128)(2,1)} custom-call(bf16[128,2048]{1,0:T(8,128)(2,1)} %bitcast.5, bf16[2048,1024]{1,0:T(8,128)(2,1)} %wg_ref.1, bf16[2048,1024]{1,0:T(8,128)(2,1)} %wv_ref.1, bf16[2048,512]{1,0:T(8,128)(2,1)} %ws_ref.1, bf16[2,16,2048]{2,1,0:T(8,128)(2,1)} %bitcast.6, bf16[1024,2048]{1,0:T(8,128)(2,1)} %wo_ref.1, f32[2,16]{1,0:T(2,128)} %bias_in.1, ...), custom_call_target="tpu_custom_call" | custom-call | tf_op jit(solution)/shard_map/layer/pallas_call | solution.py:571
  65.7 1.9 %copy.13 = bf16[1,128,2048]{2,1,0:T(8,128)(2,1)} copy(bf16[1,128,2048]{2,1,0:T(8,128)(2,1)} %bitcast.4) | data formatting | bytes 1048576

commit v6 on v5

--- a/solution.py
+++ b/solution.py
@@ -483,10 +483,7 @@
             normed[block(n), lanes(g)] = (gated * gain_ref[:, lanes(g)]).astype(BF)
         sq[n] = jnp.broadcast_to(jnp.sum(total.T, axis=0, keepdims=True), (8, BLK))
 
-    @pl.loop(0, 2)
-    def _(n):
-        gated_rows(n, jnp.where(n == 0, corner, across))
-
+    gated_rows(row * 0, corner)
     loads[11].wait()
     ones, twos, threes = [], [], []
 
@@ -500,16 +497,24 @@
         copy.start()
         twos.append(copy)
 
-    for k in range(NCOL):
-        cols = slice(k * COLS, (k + 1) * COLS)
-        part = dot(normed[0:HALF, :], wo[:, cols])
-        to_partner[0, k] = part[0:BLK].astype(BF)
+    def hand_over(k, part):
+        to_partner[0, k] = part.astype(BF)
         copy = remote(
             to_partner.at[0, k], from_partner.at[0, k], f_s.at[k], f_r.at[k], dev(frame, partner)
         )
         copy.start()
         ones.append(copy)
-        own[k] = part[BLK:]
+
+    for k in range(NCOL):
+        cols = slice(k * COLS, (k + 1) * COLS)
+        if k == 0:
+            hand_over(k, dot(normed[0:BLK, :], wo[:, cols]))
+            gated_rows(row * 0 + 1, across)
+            own[k] = dot(normed[BLK:HALF, :], wo[:, cols])
+        else:
+            part = dot(normed[0:HALF, :], wo[:, cols])
+            hand_over(k, part[0:BLK])
+            own[k] = part[BLK:]
         if k >= LAG:
             relay(k - LAG)
     for k in range(NCOL - LAG, NCOL):

time: 67.7 us -> 67.3 us (level)
  no operation moved by 1% of the time
where the time goes in v6:
time: 67.3 us; the launch traced here: 67.2 us
  Pallas kernels  65.3 us (97%)
  local copies, waits for them, and re-layouts  1.88 us (3%)
    pallas_call x1, Pallas kernels, layer(): pl.pallas_call(layer_body, name='layer', out_shape=jax.ShapeDtypeStruct((...  65.3 us
    unnamed x1, local copies, waits for them, and re-layouts  1.88 us

profile of v6, /device:TPU:1, one launch (start us, length us, event | category | flops | bytes accessed | tf_op | source)
XLA Modules:
  0.0 67.2 jit_solution(8641804943269365287)
XLA Ops:
  0.0 65.3 %layer.1 = bf16[128,2048]{1,0:T(8,128)(2,1)} custom-call(bf16[128,2048]{1,0:T(8,128)(2,1)} %bitcast.5, bf16[2048,1024]{1,0:T(8,128)(2,1)} %wg_ref.1, bf16[2048,1024]{1,0:T(8,128)(2,1)} %wv_ref.1, bf16[2048,512]{1,0:T(8,128)(2,1)} %ws_ref.1, bf16[2,16,2048]{2,1,0:T(8,128)(2,1)} %bitcast.6, bf16[1024,2048]{1,0:T(8,128)(2,1)} %wo_ref.1, f32[2,16]{1,0:T(2,128)} %bias_in.1, ...), custom_call_target="tpu_custom_call" | custom-call | tf_op jit(solution)/shard_map/layer/pallas_call | solution.py:576
  65.3 1.9 %copy.13 = bf16[1,128,2048]{2,1,0:T(8,128)(2,1)} copy(bf16[1,128,2048]{2,1,0:T(8,128)(2,1)} %bitcast.4) | data formatting | bytes 1048576
